TPU v7x, 16 devices: a 4x2x1 block of a 4x4x8 slice. The times are simulated.
16 devices in a mesh: dp: 2 (over y, z), tp: 8 (over x, core).
Axes of the slice: x: 4, y: 2, z: 1, core: 2. Of those that a mesh axis runs over, the one named last changes fastest.
The devices are a block of a 4x4x8 slice.
Arguments:
- tokens: int32 [6, 1536], P('dp'), parts along dimension 0
- positions: int32 [6, 1536], P('dp'), parts along dimension 0
- embed_table: bfloat16 [32000, 4096], P('tp')
- w_query: bfloat16 [4096, 32, 128], P(None, 'tp')
- w_key: bfloat16 [4096, 8, 128], P(None, 'tp')
- w_value: bfloat16 [4096, 8, 128], P(None, 'tp')
- w_out: bfloat16 [32, 128, 4096], P('tp')
- w_gate: bfloat16 [4096, 14336], P(None, 'tp')
- w_up: bfloat16 [4096, 14336], P(None, 'tp')
- w_down: bfloat16 [14336, 4096], P('tp')
- norm_pre_att: float32 [4096], replicated
- norm_post_att: float32 [4096], replicated
- norm_pre_ffw: float32 [4096], replicated
- norm_post_ffw: float32 [4096], replicated
Outputs:
- output: bfloat16 [6, 1536, 4096], P('dp', 'tp'), parts along dimension 0
There are 2 independent parts. A program takes and returns all parts, laid end to end along the dimension named above; an argument that names none is the same for every part.
All inputs are finite; a program needn't handle non-finite values.
Results may differ from a plain program's by a relative error of at most 0.0181964.
Values are sent between devices in bfloat16 or wider.
A program may use at most 768 MiB of HBM per device.

v0:
```python
import functools

import jax
import jax.numpy as jnp
from jax import lax
from jax.experimental import pallas as pl
from jax.experimental.pallas import tpu as pltpu
from jax.sharding import PartitionSpec as P


WINDOW = 4096
QUERY_SCALE = 256.0 ** -0.5
SOFT_CAP = 50.0
NORM_EPS = 1e-6
ROPE_BASE = 10000.0

ROW_ORDER = "000101120212100000021012111010012222202121110210221220122"


def step_order(n_batch):
    return [int(row) for row in ROW_ORDER if int(row) < n_batch]


def rms_norm(hidden, norm_scale):
    hidden = hidden.astype(jnp.float32)
    mean_sq = jnp.mean(hidden * hidden, axis=-1, keepdims=True)
    return (hidden * lax.rsqrt(mean_sq + NORM_EPS) * (1.0 + norm_scale)).astype(jnp.bfloat16)


def rope_tables(positions, head_dim):
    half_dim = head_dim // 2
    inv_freq = ROPE_BASE ** (-2.0 * jnp.arange(half_dim, dtype=jnp.float32) / head_dim)
    angles = positions.astype(jnp.float32)[:, :, None] * inv_freq
    cos_tab, sin_tab = jnp.cos(angles), jnp.sin(angles)
    return jnp.concatenate([cos_tab, cos_tab], axis=-1), jnp.concatenate([-sin_tab, sin_tab], axis=-1)


def attention_body(q_block, pos_row_ref, pos_col_ref, q_ref, k_ref, v_ref, cos_ref, sin_ref, out_ref):
    seq_len, head_dim = q_ref.shape
    half_dim = head_dim // 2

    def rope(states):
        return states * cos_ref[...] + pltpu.roll(states, half_dim, 1) * sin_ref[...]

    keys = rope(k_ref[...]).astype(jnp.bfloat16)
    values = v_ref[...].astype(jnp.bfloat16)
    queries = (rope(q_ref[...]) * QUERY_SCALE).astype(jnp.bfloat16)
    for start in range(0, seq_len, q_block):
        span = start + q_block
        scores = lax.dot_general(queries[start:span], keys[:span], (((1,), (1,)), ((), ())), preferred_element_type=jnp.float32)
        capped = SOFT_CAP * jnp.tanh(scores * (1.0 / SOFT_CAP))
        offset = pos_col_ref[start:span, :] - pos_row_ref[:, :span]
        keep_mask = (offset >= 0) & (offset < WINDOW)
        weights = jnp.where(keep_mask, jnp.exp(capped), 0.0)
        total = jnp.sum(weights, axis=-1, keepdims=True)
        probs = (weights * (1.0 / total)).astype(jnp.bfloat16)
        mix = jnp.dot(probs, values[:span], preferred_element_type=jnp.float32)
        out_ref[start:span, :] = mix.astype(jnp.bfloat16)


def local_attention(qkv, positions, cos_tab, sin_tab, n_heads, head_dim, kv_local):
    seq_len = qkv.shape[0]
    n_group = n_heads // kv_local
    whole = pl.BlockSpec((seq_len, head_dim), lambda h: (0, 0))
    flops = 2 * n_heads * seq_len * seq_len * head_dim * 2
    return pl.pallas_call(
        functools.partial(attention_body, 256),
        grid=(n_heads,),
        in_specs=[
            pl.BlockSpec((1, seq_len), lambda h: (0, 0)),
            pl.BlockSpec((seq_len, 1), lambda h: (0, 0)),
            pl.BlockSpec((seq_len, head_dim), lambda h: (0, h)),
            pl.BlockSpec((seq_len, head_dim), lambda h: (0, n_heads + h // n_group)),
            pl.BlockSpec((seq_len, head_dim), lambda h: (0, n_heads + kv_local + h // n_group)),
            whole,
            whole,
        ],
        out_specs=pl.BlockSpec((seq_len, head_dim), lambda h: (0, h)),
        out_shape=jax.ShapeDtypeStruct((seq_len, n_heads * head_dim), jnp.bfloat16),
        compiler_params=pltpu.CompilerParams(vmem_limit_bytes=40 * 1024 * 1024),
        cost_estimate=pl.CostEstimate(flops=flops, bytes_accessed=12 * seq_len * n_heads * head_dim, transcendentals=0),
        name="attention",
    )(positions[None, :], positions[:, None], qkv, qkv, qkv, cos_tab, sin_tab)


def solution(mesh):
    in_specs = (P("dp", None), P("dp", None), P("tp", None), P(None, "tp", None), P(None, "tp", None), P(None, "tp", None), P("tp", None, None), P(None, "tp"), P(None, "tp"), P("tp", None), P(None), P(None), P(None), P(None))
    n_dev = mesh.shape["tp"]
    n_chip = n_dev // 2
    to_right = [(i, (i + 2) % n_dev) for i in range(n_dev)]
    to_left = [(i, (i - 2) % n_dev) for i in range(n_dev)]
    to_partner = [(i, i ^ 1) for i in range(n_dev)]

    def layer(tokens, positions, embed_block, w_query, w_key, w_value, w_out, w_gate, w_up, w_down, norm_pre_att, norm_post_att, norm_pre_ffw, norm_post_ffw):
        dev_rank = lax.axis_index("tp")
        chip, core = dev_rank // 2, dev_rank % 2
        vocab_local, model_dim = embed_block.shape
        n_batch, seq_len = tokens.shape
        chunk = seq_len // n_dev
        half = chunk // 2
        n_heads, head_dim = w_query.shape[1], w_query.shape[2]
        kv_local = w_key.shape[1]

        clock = []

        def step(fn, *args):
            leaves, tree = jax.tree.flatten(args)
            if clock:
                leaves = lax.optimization_barrier((leaves, list(clock)))[0]
            result = fn(*jax.tree.unflatten(tree, leaves))
            clock[:] = jax.tree.leaves(result)
            return result

        def shift(rows, perm):
            return lax.ppermute(rows, "tp", perm)

        def by_parity(rows, parity):
            split = rows.reshape((n_chip, 2, chunk) + rows.shape[1:])
            picked = lax.dynamic_index_in_dim(split, parity, 1, keepdims=False)
            return picked.reshape((n_chip * chunk,) + rows.shape[1:])

        def ring_steps(own, from_partner, pair_sum, finish):
            def pair(ahead, upper, own, from_partner):
                start = ((chip + ahead) % n_chip) * chunk + (half if upper else 0)
                mine = lax.dynamic_slice_in_dim(own, start, half, 0)
                theirs = lax.dynamic_slice_in_dim(from_partner, start, half, 0)
                return pair_sum(mine, theirs, start, half)

            def first(own, theirs):
                order = ((2, False), (2, True), (1, True), (n_chip - 1, False))
                return [pair(ahead, upper, own, theirs).astype(jnp.bfloat16) for ahead, upper in order]

            sends = step(first, own, from_partner)
            far_low, far_high, left_high, right_low = [shift(part, perm) for part, perm in zip(sends, (to_right, to_left, to_right, to_left))]
            yield

            def second(own, theirs, low, high):
                low = pair(1, False, own, theirs) + low.astype(jnp.float32)
                high = pair(n_chip - 1, True, own, theirs) + high.astype(jnp.float32)
                return low.astype(jnp.bfloat16), high.astype(jnp.bfloat16)

            low, high = step(second, own, from_partner, far_low, far_high)
            left_low, right_high = shift(low, to_right), shift(high, to_left)
            yield

            def last(own, theirs, *arrived):
                right_low, left_low, left_high, right_high = [part.astype(jnp.float32) for part in arrived]
                low = pair(0, False, own, theirs) + right_low + left_low
                high = pair(0, True, own, theirs) + left_high + right_high
                return finish(jnp.concatenate([low, high], axis=0).astype(jnp.bfloat16))

            result = step(last, own, from_partner, right_low, left_low, left_high, right_high)
            yield
            return result

        normalizer = jnp.sqrt(jnp.float32(model_dim)).astype(jnp.bfloat16)
        first_id = dev_rank * vocab_local
        partner_first_id = (dev_rank + 1 - 2 * core) * vocab_local

        def lookup(ids):
            return embed_block.at[jnp.mod(ids - first_id, vocab_local)].get(mode="promise_in_bounds")

        w_qkv = jnp.concatenate([w.reshape(model_dim, -1) for w in (w_query, w_key, w_value)], axis=1)
        w_out_flat = w_out.reshape(-1, model_dim)
        cos_tab, sin_tab = rope_tables(positions, head_dim)

        def project_out(rows):
            return jnp.dot(rows, w_out_flat, preferred_element_type=jnp.float32).astype(jnp.bfloat16)

        def project_down(rows):
            return jnp.dot(rows, w_down, preferred_element_type=jnp.float32).astype(jnp.bfloat16)

        def add_sums(mine, theirs, start, size):
            return mine.astype(jnp.float32) + theirs.astype(jnp.float32)

        def row_steps(b):
            own_ids, other_ids = by_parity(tokens[b], core), by_parity(tokens[b], 1 - core)
            other = step(lookup, other_ids)
            from_partner = shift(other, to_partner)
            yield
            own = step(lookup, own_ids)
            yield

            def pick_row(mine, theirs, start, size):
                ids = lax.dynamic_slice_in_dim(own_ids, start, size, 0)[:, None]
                from_mine = (ids >= first_id) & (ids < first_id + vocab_local)
                from_theirs = (ids >= partner_first_id) & (ids < partner_first_id + vocab_local)
                zero = jnp.zeros((), jnp.bfloat16)
                return jnp.where(from_mine, mine * normalizer, jnp.where(from_theirs, theirs * normalizer, zero)).astype(jnp.float32)

            embeds, normed = yield from ring_steps(own, from_partner, pick_row, lambda e: (e, rms_norm(e, norm_pre_att)))
            attn_in = lax.all_gather(normed, "tp", axis=0, tiled=True)
            qkv = step(lambda rows: jnp.dot(rows, w_qkv, preferred_element_type=jnp.float32), attn_in)
            yield
            att_mix = step(lambda rows: local_attention(rows, positions[b], cos_tab[b], sin_tab[b], n_heads, head_dim, kv_local), qkv)
            yield
            other = step(lambda rows: project_out(by_parity(rows, 1 - core)), att_mix)
            from_partner = shift(other, to_partner)
            yield
            own = step(lambda rows: project_out(by_parity(rows, core)), att_mix)
            yield

            def after_attention(att_proj):
                resid = (embeds.astype(jnp.float32) + rms_norm(att_proj, norm_post_att).astype(jnp.float32)).astype(jnp.bfloat16)
                return resid, rms_norm(resid, norm_pre_ffw)

            resid_one, normed = yield from ring_steps(own, from_partner, add_sums, after_attention)
            mlp_in = lax.all_gather(normed, "tp", axis=0, tiled=True)
            gate_pre = step(lambda rows: jnp.dot(rows, w_gate, preferred_element_type=jnp.float32), mlp_in)
            yield

            def activate(rows, gate_pre):
                up_proj = jnp.dot(rows, w_up, preferred_element_type=jnp.float32)
                return (jax.nn.gelu(gate_pre, approximate=True) * up_proj).astype(jnp.bfloat16)

            ffn_act = step(activate, mlp_in, gate_pre)
            yield
            other = step(lambda rows: project_down(by_parity(rows, 1 - core)), ffn_act)
            from_partner = shift(other, to_partner)
            yield
            own = step(lambda rows: project_down(by_parity(rows, core)), ffn_act)
            yield

            def after_ffw(down_proj):
                return (resid_one.astype(jnp.float32) + rms_norm(down_proj, norm_post_ffw).astype(jnp.float32)).astype(jnp.bfloat16)

            outs[b] = yield from ring_steps(own, from_partner, add_sums, after_ffw)

        outs = [None] * n_batch
        rows = [row_steps(b) for b in range(n_batch)]
        for b in step_order(n_batch):
            next(rows[b], None)
        for row in rows:
            for _ in row:
                pass
        return jnp.stack(outs)

    return jax.shard_map(layer, mesh=mesh, in_specs=in_specs, out_specs=P("dp", "tp", None), check_vma=False)
```

profile of v0, /device:TPU:112, one launch (start us, length us, event | category | flops | bytes accessed | tf_op | source)
XLA Modules:
  0.0 1038.3 jit_solution(6859267303675962708)
XLA Ops:
  7.7 14.5 %gather_fusion = bf16[768,4096]{1,0:T(8,128)(2,1)} fusion(bf16[4000,4096]{1,0:T(8,128)(2,1)} %param.16, s32[1024]{0:T(1024)S(1)} %pad_clamp_fusion.5), kind=kCustom, calls=%fused_computation | custom fusion | bytes 12585984 | tf_op jit(solution)/shard_map/gather | solution.py:161
  22.3 14.5 %gather_fusion.1 = bf16[768,4096]{1,0:T(8,128)(2,1)} fusion(bf16[4000,4096]{1,0:T(8,128)(2,1)} %param.16, s32[1024]{0:T(1024)S(1)} %pad_clamp_fusion.4), kind=kCustom, calls=%fused_computation.1 | custom fusion | bytes 12585984 | tf_op jit(solution)/shard_map/gather | solution.py:161
  41.9 14.8 %gather_fusion.2 = bf16[768,4096]{1,0:T(8,128)(2,1)} fusion(bf16[4000,4096]{1,0:T(8,128)(2,1)} %param.16, s32[1024]{0:T(1024)S(1)} %pad_clamp_fusion.3), kind=kCustom, calls=%fused_computation.2 | custom fusion | bytes 12585984 | tf_op jit(solution)/shard_map/gather | solution.py:161
  63.5 16.0 %collective-permute-done.2 = bf16[96,4096]{1,0:T(8,128)(2,1)S(1)} collective-permute-done((bf16[96,4096]{1,0:T(8,128)(2,1)S(1)}, bf16[96,4096]{1,0:T(8,128)(2,1)S(1)}, u32[]{:S(2)}, u32[]{:S(2)}) %collective-permute-start.2) | collective-permute-done | bytes 786464 | tf_op jit(solution)/shard_map/ppermute | solution.py:115
  87.8 14.5 %gather_fusion.3 = bf16[768,4096]{1,0:T(8,128)(2,1)} fusion(bf16[4000,4096]{1,0:T(8,128)(2,1)} %param.16, s32[1024]{0:T(1024)S(1)} %pad_clamp_fusion.2), kind=kCustom, calls=%fused_computation.3 | custom fusion | bytes 12585984 | tf_op jit(solution)/shard_map/gather | solution.py:161
  107.0 14.9 %gather_fusion.4 = bf16[768,4096]{1,0:T(8,128)(2,1)} fusion(bf16[4000,4096]{1,0:T(8,128)(2,1)} %param.16, s32[1024]{0:T(1024)S(1)} %pad_clamp_fusion.1), kind=kCustom, calls=%fused_computation.4 | custom fusion | bytes 12585984 | tf_op jit(solution)/shard_map/gather | solution.py:161
  134.7 15.2 %gather_fusion.5 = bf16[768,4096]{1,0:T(8,128)(2,1)} fusion(bf16[4000,4096]{1,0:T(8,128)(2,1)} %param.16, s32[1024]{0:T(1024)S(1)} %pad_clamp_fusion), kind=kCustom, calls=%fused_computation.5 | custom fusion | bytes 12585984 | tf_op jit(solution)/shard_map/gather | solution.py:161
  150.0 9.7 collective-permute-done.10
  175.8 22.6 %collective-permute-done.12 = bf16[96,4096]{1,0:T(8,128)(2,1)} collective-permute-done((bf16[96,4096]{1,0:T(8,128)(2,1)S(1)}, bf16[96,4096]{1,0:T(8,128)(2,1)}, u32[]{:S(2)}, u32[]{:S(2)}) %collective-permute-start.12) | collective-permute-done | bytes 786464 | tf_op jit(solution)/shard_map/ppermute | solution.py:115
  198.4 32.7 %collective-permute-done.11 = bf16[96,4096]{1,0:T(8,128)(2,1)S(1)} collective-permute-done((bf16[96,4096]{1,0:T(8,128)(2,1)S(1)}, bf16[96,4096]{1,0:T(8,128)(2,1)S(1)}, u32[]{:S(2)}, u32[]{:S(2)}) %collective-permute-start.11) | collective-permute-done | bytes 786464 | tf_op jit(solution)/shard_map/ppermute | solution.py:115
  244.7 8.6 multiply_sine_fusion
  255.7 15.0 %fusion.79.q_ref.k_ref.v_ref = f32[1536,768]{1,0:T(8,128)S(1)} fusion(bf16[1536,4096]{1,0:T(8,128)(2,1)} %all-gather.7.cloned.1.call-done, bf16[4096,128]{1,0:T(8,128)(2,1)} %bitcast.164, bf16[4096,128]{1,0:T(8,128)(2,1)} %bitcast.167, bf16[4096,512]{1,0:T(8,128)(2,1)} %bitcast.143), kind=kOutput, calls=%fused_computation.341 | convolution fusion | flops 9682550784 | bytes 23592960 | tf_op jit(solution)/shard_map/dot_general | solution.py:193
  270.7 19.6 %attention.3 = bf16[1536,512]{1,0:T(8,128)(2,1)S(1)} custom-call(s32[1,1536]{1,0:T(1,128)S(1)} %get-tuple-element.382.pos_row_ref, s32[1536,1]{1,0:T(8,128)S(1)} %copy-done.3, f32[1536,768]{1,0:T(8,128)S(1)} %fusion.79.q_ref.k_ref.v_ref, f32[1536,768]{1,0:T(8,128)S(1)} %fusion.79.q_ref.k_ref.v_ref, f32[1536,768]{1,0:T(8,128)S(1)} %fusion.79.q_ref.k_ref.v_ref, ...), custom_call_target="tpu_custom_call" | custom-call | flops 4831838208 | bytes 9437184 | tf_op jit(solution)/shard_map/attention/pallas_call | solution.py:66
  297.9 7.5 collective-permute-done.15
  313.7 14.5 %collective-permute-done.17 = bf16[96,4096]{1,0:T(8,128)(2,1)S(1)} collective-permute-done((bf16[96,4096]{1,0:T(8,128)(2,1)S(1)}, bf16[96,4096]{1,0:T(8,128)(2,1)S(1)}, u32[]{:S(2)}, u32[]{:S(2)}) %collective-permute-start.17) | collective-permute-done | bytes 786464 | tf_op jit(solution)/shard_map/ppermute | solution.py:115
  330.2 14.9 %collective-permute-done.22 = bf16[96,4096]{1,0:T(8,128)(2,1)S(1)} collective-permute-done((bf16[96,4096]{1,0:T(8,128)(2,1)S(1)}, bf16[96,4096]{1,0:T(8,128)(2,1)S(1)}, u32[]{:S(2)}, u32[]{:S(2)}) %collective-permute-start.22) | collective-permute-done | bytes 786464 | tf_op jit(solution)/shard_map/ppermute | solution.py:115
  349.3 16.2 %fusion.78.q_ref.k_ref.v_ref = f32[1536,768]{1,0:T(8,128)} fusion(bf16[1536,4096]{1,0:T(8,128)(2,1)} %all-gather.9.cloned.1.call-done, bf16[4096,128]{1,0:T(8,128)(2,1)} %bitcast.165, bf16[4096,128]{1,0:T(8,128)(2,1)} %bitcast.168, bf16[4096,512]{1,0:T(8,128)(2,1)} %bitcast.144), kind=kOutput, calls=%fused_computation.340 | convolution fusion | flops 9682550784 | bytes 23592960 | tf_op jit(solution)/shard_map/dot_general | solution.py:193
  365.5 12.5 %collective-permute-done.19 = bf16[96,4096]{1,0:T(8,128)(2,1)} collective-permute-done((bf16[96,4096]{1,0:T(8,128)(2,1)}, bf16[96,4096]{1,0:T(8,128)(2,1)}, u32[]{:S(2)}, u32[]{:S(2)}) %collective-permute-start.19) | collective-permute-done | bytes 786464 | tf_op jit(solution)/shard_map/ppermute | solution.py:115
  399.1 19.3 %attention.4 = bf16[1536,512]{1,0:T(8,128)(2,1)S(1)} custom-call(s32[1,1536]{1,0:T(1,128)S(1)} %get-tuple-element.384.pos_row_ref, s32[1536,1]{1,0:T(8,128)S(1)} %copy-done.4, f32[1536,768]{1,0:T(8,128)S(1)} %copy-done, f32[1536,768]{1,0:T(8,128)S(1)} %copy-done, f32[1536,768]{1,0:T(8,128)S(1)} %copy-done, f32[1536,128]{1,0:T(8,128)S(1)} %copy-done.2, ...), custom_call_target="tpu_custom_call" | custom-call | flops 4831838208 | bytes 9437184 | tf_op jit(solution)/shard_map/attention/pallas_call | solution.py:66
  422.4 31.5 %collective-permute-done.25 = bf16[96,4096]{1,0:T(8,128)(2,1)} collective-permute-done((bf16[96,4096]{1,0:T(8,128)(2,1)}, bf16[96,4096]{1,0:T(8,128)(2,1)}, u32[]{:S(2)}, u32[]{:S(2)}) %collective-permute-start.25) | collective-permute-done | bytes 786464 | tf_op jit(solution)/shard_map/ppermute | solution.py:115
  461.1 7.5 convolution_convert_fusion.3
  468.8 6.2 convolution_convert_fusion.2
  475.0 5.2 collective-permute-done.28
  489.8 31.5 %fusion.83 = f32[1536,1792]{1,0:T(8,128)} fusion(bf16[1536,4096]{1,0:T(8,128)(2,1)} %all-gather.11.cloned.1.call-done, bf16[4096,1792]{1,0:T(8,128)(2,1)} %param.21), kind=kOutput, calls=%fused_computation.342 | convolution fusion | flops 22548578304 | bytes 38273024 | tf_op jit(solution)/shard_map/dot_general | solution.py:209
  529.8 31.4 %fusion.8 = bf16[1536,1792]{1,0:T(8,128)(2,1)S(1)} fusion(f32[1536,1792]{1,0:T(8,128)} %fusion.83, bf16[1536,4096]{1,0:T(8,128)(2,1)} %all-gather.11.cloned.1.call-done, bf16[4096,1792]{1,0:T(8,128)(2,1)} %param.22), kind=kOutput, calls=%fused_computation.17 | convolution fusion | flops 22576103424 | bytes 43778048 | tf_op jit(solution)/shard_map/dot_general | solution.py:213
  561.4 18.3 %convolution_convert_fusion.11 = bf16[768,4096]{1,0:T(8,128)(2,1)} fusion(bf16[768,1792]{1,0:T(8,128)(2,1)S(1)} %bitcast.150, bf16[1792,4096]{1,0:T(8,128)(2,1)} %param.23), kind=kOutput, calls=%fused_computation.47 | convolution fusion | flops 11277434880 | bytes 23724032 | tf_op jit(solution)/shard_map/dot_general | solution.py:171
  579.7 10.0 collective-permute-done.32
  597.0 14.9 %fusion.77.q_ref.k_ref.v_ref = f32[1536,768]{1,0:T(8,128)S(1)} fusion(bf16[1536,4096]{1,0:T(8,128)(2,1)} %all-gather.13.cloned.1.call-done, bf16[4096,128]{1,0:T(8,128)(2,1)} %bitcast.166, bf16[4096,128]{1,0:T(8,128)(2,1)} %bitcast.169, bf16[4096,512]{1,0:T(8,128)(2,1)} %bitcast.145), kind=kOutput, calls=%fused_computation.339 | convolution fusion | flops 9682550784 | bytes 23592960 | tf_op jit(solution)/shard_map/dot_general | solution.py:193
  611.9 19.2 %attention.5 = bf16[1536,512]{1,0:T(8,128)(2,1)S(1)} custom-call(s32[1,1536]{1,0:T(1,128)S(1)} %get-tuple-element.383.pos_row_ref, s32[1536,1]{1,0:T(8,128)S(1)} %copy.17.pos_col_ref, f32[1536,768]{1,0:T(8,128)S(1)} %fusion.77.q_ref.k_ref.v_ref, f32[1536,768]{1,0:T(8,128)S(1)} %fusion.77.q_ref.k_ref.v_ref, f32[1536,768]{1,0:T(8,128)S(1)} %fusion.77.q_ref.k_ref.v_ref, ...), custom_call_target="tpu_custom_call" | custom-call | flops 4831838208 | bytes 9437184 | tf_op jit(solution)/shard_map/attention/pallas_call | solution.py:66
  639.1 7.1 collective-permute-done.35
  653.0 16.5 %convolution_convert_fusion.10 = bf16[768,4096]{1,0:T(8,128)(2,1)} fusion(bf16[768,1792]{1,0:T(8,128)(2,1)S(1)} %bitcast.147, bf16[1792,4096]{1,0:T(8,128)(2,1)} %param.23), kind=kOutput, calls=%fused_computation.46 | convolution fusion | flops 11277434880 | bytes 23724032 | tf_op jit(solution)/shard_map/dot_general | solution.py:171
  669.5 6.7 collective-permute-done.37
  681.4 31.6 %fusion.84 = f32[1536,1792]{1,0:T(8,128)} fusion(bf16[1536,4096]{1,0:T(8,128)(2,1)} %all-gather.15.cloned.1.call-done, bf16[4096,1792]{1,0:T(8,128)(2,1)} %param.21), kind=kOutput, calls=%fused_computation.343 | convolution fusion | flops 22548578304 | bytes 38273024 | tf_op jit(solution)/shard_map/dot_general | solution.py:209
  719.9 32.6 %fusion.17 = bf16[1536,1792]{1,0:T(8,128)(2,1)S(1)} fusion(f32[1536,1792]{1,0:T(8,128)} %fusion.84, bf16[1536,4096]{1,0:T(8,128)(2,1)} %all-gather.15.cloned.1.call-done, bf16[4096,1792]{1,0:T(8,128)(2,1)} %param.22), kind=kOutput, calls=%fused_computation.26 | convolution fusion | flops 22576103424 | bytes 43778048 | tf_op jit(solution)/shard_map/dot_general | solution.py:213
  752.7 16.6 %convolution_convert_fusion.9 = bf16[768,4096]{1,0:T(8,128)(2,1)} fusion(bf16[768,1792]{1,0:T(8,128)(2,1)S(1)} %bitcast.151, bf16[1792,4096]{1,0:T(8,128)(2,1)} %param.23), kind=kOutput, calls=%fused_computation.45 | convolution fusion | flops 11277434880 | bytes 23724032 | tf_op jit(solution)/shard_map/dot_general | solution.py:171
  770.0 17.2 %convolution_convert_fusion.8 = bf16[768,4096]{1,0:T(8,128)(2,1)} fusion(bf16[768,1792]{1,0:T(8,128)(2,1)S(1)} %bitcast.148, bf16[1792,4096]{1,0:T(8,128)(2,1)} %param.23), kind=kOutput, calls=%fused_computation.44 | convolution fusion | flops 11277434880 | bytes 23724032 | tf_op jit(solution)/shard_map/dot_general | solution.py:171
  794.0 31.8 %fusion.85 = f32[1536,1792]{1,0:T(8,128)} fusion(bf16[1536,4096]{1,0:T(8,128)(2,1)} %all-gather.17.cloned.1.call-done, bf16[4096,1792]{1,0:T(8,128)(2,1)} %param.21), kind=kOutput, calls=%fused_computation.344 | convolution fusion | flops 22548578304 | bytes 38273024 | tf_op jit(solution)/shard_map/dot_general | solution.py:209
  825.9 5.1 add_convert_fusion.22
  834.4 32.1 %fusion.26 = bf16[1536,1792]{1,0:T(8,128)(2,1)} fusion(f32[1536,1792]{1,0:T(8,128)} %fusion.85, bf16[1536,4096]{1,0:T(8,128)(2,1)} %all-gather.17.cloned.1.call-done, bf16[4096,1792]{1,0:T(8,128)(2,1)} %param.22), kind=kOutput, calls=%fused_computation.35 | convolution fusion | flops 22576103424 | bytes 43778048 | tf_op jit(solution)/shard_map/dot_general | solution.py:213
  868.4 16.7 %convolution_convert_fusion.7 = bf16[768,4096]{1,0:T(8,128)(2,1)} fusion(bf16[768,1792]{1,0:T(8,128)(2,1)S(1)} %bitcast.149, bf16[1792,4096]{1,0:T(8,128)(2,1)} %param.23), kind=kOutput, calls=%fused_computation.43 | convolution fusion | flops 11277434880 | bytes 23724032 | tf_op jit(solution)/shard_map/dot_general | solution.py:171
  890.5 16.6 %collective-permute-done.50 = bf16[96,4096]{1,0:T(8,128)(2,1)S(1)} collective-permute-done((bf16[96,4096]{1,0:T(8,128)(2,1)}, bf16[96,4096]{1,0:T(8,128)(2,1)S(1)}, u32[]{:S(2)}, u32[]{:S(2)}) %collective-permute-start.50) | collective-permute-done | bytes 786464 | tf_op jit(solution)/shard_map/ppermute | solution.py:115
  916.1 16.6 %convolution_convert_fusion.6 = bf16[768,4096]{1,0:T(8,128)(2,1)} fusion(bf16[768,1792]{1,0:T(8,128)(2,1)S(1)} %bitcast.146, bf16[1792,4096]{1,0:T(8,128)(2,1)} %param.23), kind=kOutput, calls=%fused_computation.42 | convolution fusion | flops 11277434880 | bytes 23724032 | tf_op jit(solution)/shard_map/dot_general | solution.py:171
  934.8 6.1 collective-permute-done.54
  950.6 6.4 collective-permute-done.43
  960.7 13.8 %collective-permute-done.47 = bf16[96,4096]{1,0:T(8,128)(2,1)S(1)} collective-permute-done((bf16[96,4096]{1,0:T(8,128)(2,1)}, bf16[96,4096]{1,0:T(8,128)(2,1)S(1)}, u32[]{:S(2)}, u32[]{:S(2)}) %collective-permute-start.47) | collective-permute-done | bytes 786464 | tf_op jit(solution)/shard_map/ppermute | solution.py:115
  976.0 15.3 %collective-permute-done.58 = bf16[96,4096]{1,0:T(8,128)(2,1)S(1)} collective-permute-done((bf16[96,4096]{1,0:T(8,128)(2,1)}, bf16[96,4096]{1,0:T(8,128)(2,1)S(1)}, u32[]{:S(2)}, u32[]{:S(2)}) %collective-permute-start.58) | collective-permute-done | bytes 786464 | tf_op jit(solution)/shard_map/ppermute | solution.py:115
  996.9 5.5 add_convert_fusion.4
  1008.2 16.3 %collective-permute-done.60 = bf16[96,4096]{1,0:T(8,128)(2,1)S(1)} collective-permute-done((bf16[96,4096]{1,0:T(8,128)(2,1)S(1)}, bf16[96,4096]{1,0:T(8,128)(2,1)S(1)}, u32[]{:S(2)}, u32[]{:S(2)}) %collective-permute-start.60) | collective-permute-done | bytes 786464 | tf_op jit(solution)/shard_map/ppermute | solution.py:115
  (386 shorter events, 239.2 us)
Async XLA Ops:
  6.5 249.2 %all-gather.7.cloned.1.call-start = ((), (), s32[]{:S(2)}) async-start(), calls=%async_computation | async-start | bytes 14155776 | tf_op jit(solution)/shard_map/all_gather | solution.py:192
  56.7 45.7 %collective-permute-start.7 = (bf16[768,4096]{1,0:T(8,128)(2,1)}, bf16[768,4096]{1,0:T(8,128)(2,1)}, u32[]{:S(2)}, u32[]{:S(2)}) collective-permute-start(bf16[768,4096]{1,0:T(8,128)(2,1)} %gather_fusion.2), channel_id=1, source_target_pairs={{0,1},{1,0},{2,3},{3,2},{4,5},{5,4},{6,7},{7,6},{8,9},{9,8},{10,11... | collective-permute-start | bytes 18874376 | tf_op jit(solution)/shard_map/ppermute | solution.py:115
  61.4 60.5 %collective-permute-start.1 = (bf16[96,4096]{1,0:T(8,128)(2,1)}, bf16[96,4096]{1,0:T(8,128)(2,1)}, u32[]{:S(2)}, u32[]{:S(2)}) collective-permute-start(bf16[96,4096]{1,0:T(8,128)(2,1)} %get-tuple-element.367), channel_id=1, source_target_pairs={{0,6},{1,7},{2,0},{3,1},{4,2},{5,3},{6,4},{7,5},{8,14},{9,15},{10,... | collective-permute-start | bytes 2359304 | tf_op jit(solution)/shard_map/ppermute | solution.py:115
  63.5 58.4 %collective-permute-start.5 = (bf16[96,4096]{1,0:T(8,128)(2,1)S(1)}, bf16[96,4096]{1,0:T(8,128)(2,1)}, u32[]{:S(2)}, u32[]{:S(2)}) collective-permute-start(bf16[96,4096]{1,0:T(8,128)(2,1)S(1)} %get-tuple-element.364), channel_id=1, source_target_pairs={{0,2},{1,3},{2,4},{3,5},{4,6},{5,7},{6,0},{7,1},{8,10},{9,11},{10,... | collective-permute-start | bytes 2359304 | tf_op jit(solution)/shard_map/ppermute | solution.py:115
  84.5 37.4 %collective-permute-start.4 = (bf16[96,4096]{1,0:T(8,128)(2,1)}, bf16[96,4096]{1,0:T(8,128)(2,1)}, u32[]{:S(2)}, u32[]{:S(2)}) collective-permute-start(bf16[96,4096]{1,0:T(8,128)(2,1)} %get-tuple-element.363), channel_id=1, source_target_pairs={{0,2},{1,3},{2,4},{3,5},{4,6},{5,7},{6,0},{7,1},{8,10},{9,11},{10,... | collective-permute-start | bytes 2359304 | tf_op jit(solution)/shard_map/ppermute | solution.py:115
  86.2 35.8 %collective-permute-start.6 = (bf16[96,4096]{1,0:T(8,128)(2,1)}, bf16[96,4096]{1,0:T(8,128)(2,1)}, u32[]{:S(2)}, u32[]{:S(2)}) collective-permute-start(bf16[96,4096]{1,0:T(8,128)(2,1)} %get-tuple-element.362), channel_id=1, source_target_pairs={{0,6},{1,7},{2,0},{3,1},{4,2},{5,3},{6,4},{7,5},{8,14},{9,15},{10,... | collective-permute-start | bytes 2359304 | tf_op jit(solution)/shard_map/ppermute | solution.py:115
  128.9 220.3 %all-gather.9.cloned.1.call-start = ((), (), s32[]{:S(2)}) async-start(), calls=%async_computation.1 | async-start | bytes 14155776 | tf_op jit(solution)/shard_map/all_gather | solution.py:192
  129.0 42.8 %collective-permute-start.14 = (bf16[768,4096]{1,0:T(8,128)(2,1)}, bf16[768,4096]{1,0:T(8,128)(2,1)}, u32[]{:S(2)}, u32[]{:S(2)}) collective-permute-start(bf16[768,4096]{1,0:T(8,128)(2,1)} %gather_fusion.4), channel_id=1, source_target_pairs={{0,1},{1,0},{2,3},{3,2},{4,5},{5,4},{6,7},{7,6},{8,9},{9,8},{10,11... | collective-permute-start | bytes 18874376 | tf_op jit(solution)/shard_map/ppermute | solution.py:115
  130.7 34.0 %collective-permute-start.9 = (bf16[96,4096]{1,0:T(8,128)(2,1)S(1)}, bf16[96,4096]{1,0:T(8,128)(2,1)}, u32[]{:S(2)}, u32[]{:S(2)}) collective-permute-start(bf16[96,4096]{1,0:T(8,128)(2,1)S(1)} %get-tuple-element.361), channel_id=1, source_target_pairs={{0,2},{1,3},{2,4},{3,5},{4,6},{5,7},{6,0},{7,1},{8,10},{9,11},{10,... | collective-permute-start | bytes 2359304 | tf_op jit(solution)/shard_map/ppermute | solution.py:115
  131.4 67.0 %collective-permute-start.12 = (bf16[96,4096]{1,0:T(8,128)(2,1)S(1)}, bf16[96,4096]{1,0:T(8,128)(2,1)}, u32[]{:S(2)}, u32[]{:S(2)}) collective-permute-start(bf16[96,4096]{1,0:T(8,128)(2,1)S(1)} %get-tuple-element.359), channel_id=1, source_target_pairs={{0,2},{1,3},{2,4},{3,5},{4,6},{5,7},{6,0},{7,1},{8,10},{9,11},{10,... | collective-permute-start | bytes 2359304 | tf_op jit(solution)/shard_map/ppermute | solution.py:115
  131.9 66.5 %collective-permute-start.8 = (bf16[96,4096]{1,0:T(8,128)(2,1)S(1)}, bf16[96,4096]{1,0:T(8,128)(2,1)}, u32[]{:S(2)}, u32[]{:S(2)}) collective-permute-start(bf16[96,4096]{1,0:T(8,128)(2,1)S(1)} %get-tuple-element.358), channel_id=1, source_target_pairs={{0,6},{1,7},{2,0},{3,1},{4,2},{5,3},{6,4},{7,5},{8,14},{9,15},{10,... | collective-permute-start | bytes 2359304 | tf_op jit(solution)/shard_map/ppermute | solution.py:115
  168.4 62.7 %collective-permute-start.11 = (bf16[96,4096]{1,0:T(8,128)(2,1)S(1)}, bf16[96,4096]{1,0:T(8,128)(2,1)S(1)}, u32[]{:S(2)}, u32[]{:S(2)}) collective-permute-start(bf16[96,4096]{1,0:T(8,128)(2,1)S(1)} %get-tuple-element.355), channel_id=1, source_target_pairs={{0,2},{1,3},{2,4},{3,5},{4,6},{5,7},{6,0},{7,1},{8,10},{9,11},{10,... | collective-permute-start | bytes 2359304 | tf_op jit(solution)/shard_map/ppermute | solution.py:115
  168.6 62.6 %collective-permute-start.13 = (bf16[96,4096]{1,0:T(8,128)(2,1)S(1)}, bf16[96,4096]{1,0:T(8,128)(2,1)S(1)}, u32[]{:S(2)}, u32[]{:S(2)}) collective-permute-start(bf16[96,4096]{1,0:T(8,128)(2,1)S(1)} %get-tuple-element.354), channel_id=1, source_target_pairs={{0,6},{1,7},{2,0},{3,1},{4,2},{5,3},{6,4},{7,5},{8,14},{9,15},{10,... | collective-permute-start | bytes 2359304 | tf_op jit(solution)/shard_map/ppermute | solution.py:115
  237.9 251.9 %all-gather.11.cloned.1.call-start = ((), (), s32[]{:S(2)}) async-start(), calls=%async_computation.2 | async-start | bytes 14155776 | tf_op jit(solution)/shard_map/all_gather | solution.py:208
  310.5 34.6 %collective-permute-start.22 = (bf16[96,4096]{1,0:T(8,128)(2,1)S(1)}, bf16[96,4096]{1,0:T(8,128)(2,1)S(1)}, u32[]{:S(2)}, u32[]{:S(2)}) collective-permute-start(bf16[96,4096]{1,0:T(8,128)(2,1)S(1)} %copy-done.46), channel_id=1, source_target_pairs={{0,2},{1,3},{2,4},{3,5},{4,6},{5,7},{6,0},{7,1},{8,10},{9,11},{10,... | collective-permute-start | bytes 2359304 | tf_op jit(solution)/shard_map/ppermute | solution.py:115
  310.5 34.6 %collective-permute-start.23 = (bf16[96,4096]{1,0:T(8,128)(2,1)S(1)}, bf16[96,4096]{1,0:T(8,128)(2,1)S(1)}, u32[]{:S(2)}, u32[]{:S(2)}) collective-permute-start(bf16[96,4096]{1,0:T(8,128)(2,1)S(1)} %copy-done.45), channel_id=1, source_target_pairs={{0,6},{1,7},{2,0},{3,1},{4,2},{5,3},{6,4},{7,5},{8,14},{9,15},{10,... | collective-permute-start | bytes 2359304 | tf_op jit(solution)/shard_map/ppermute | solution.py:115
  313.7 51.8 %collective-permute-start.16 = (bf16[96,4096]{1,0:T(8,128)(2,1)S(1)}, bf16[96,4096]{1,0:T(8,128)(2,1)}, u32[]{:S(2)}, u32[]{:S(2)}) collective-permute-start(bf16[96,4096]{1,0:T(8,128)(2,1)S(1)} %get-tuple-element.344), channel_id=1, source_target_pairs={{0,6},{1,7},{2,0},{3,1},{4,2},{5,3},{6,4},{7,5},{8,14},{9,15},{10,... | collective-permute-start | bytes 2359304 | tf_op jit(solution)/shard_map/ppermute | solution.py:115
  328.2 37.3 %collective-permute-start.20 = (bf16[96,4096]{1,0:T(8,128)(2,1)S(1)}, bf16[96,4096]{1,0:T(8,128)(2,1)}, u32[]{:S(2)}, u32[]{:S(2)}) collective-permute-start(bf16[96,4096]{1,0:T(8,128)(2,1)S(1)} %get-tuple-element.345), channel_id=1, source_target_pairs={{0,2},{1,3},{2,4},{3,5},{4,6},{5,7},{6,0},{7,1},{8,10},{9,11},{10,... | collective-permute-start | bytes 2359304 | tf_op jit(solution)/shard_map/ppermute | solution.py:115
  330.2 47.9 %collective-permute-start.19 = (bf16[96,4096]{1,0:T(8,128)(2,1)}, bf16[96,4096]{1,0:T(8,128)(2,1)}, u32[]{:S(2)}, u32[]{:S(2)}) collective-permute-start(bf16[96,4096]{1,0:T(8,128)(2,1)} %get-tuple-element.343), channel_id=1, source_target_pairs={{0,2},{1,3},{2,4},{3,5},{4,6},{5,7},{6,0},{7,1},{8,10},{9,11},{10,... | collective-permute-start | bytes 2359304 | tf_op jit(solution)/shard_map/ppermute | solution.py:115
  385.2 211.8 %all-gather.13.cloned.1.call-start = ((), (), s32[]{:S(2)}) async-start(), calls=%async_computation.3 | async-start | bytes 14155776 | tf_op jit(solution)/shard_map/all_gather | solution.py:192
  388.3 34.1 %collective-permute-start.26 = (bf16[96,4096]{1,0:T(8,128)(2,1)}, bf16[96,4096]{1,0:T(8,128)(2,1)}, u32[]{:S(2)}, u32[]{:S(2)}) collective-permute-start(bf16[96,4096]{1,0:T(8,128)(2,1)} %get-tuple-element.350), channel_id=1, source_target_pairs={{0,2},{1,3},{2,4},{3,5},{4,6},{5,7},{6,0},{7,1},{8,10},{9,11},{10,... | collective-permute-start | bytes 2359304 | tf_op jit(solution)/shard_map/ppermute | solution.py:115
  388.3 65.6 %collective-permute-start.25 = (bf16[96,4096]{1,0:T(8,128)(2,1)}, bf16[96,4096]{1,0:T(8,128)(2,1)}, u32[]{:S(2)}, u32[]{:S(2)}) collective-permute-start(bf16[96,4096]{1,0:T(8,128)(2,1)} %get-tuple-element.341), channel_id=1, source_target_pairs={{0,2},{1,3},{2,4},{3,5},{4,6},{5,7},{6,0},{7,1},{8,10},{9,11},{10,... | collective-permute-start | bytes 2359304 | tf_op jit(solution)/shard_map/ppermute | solution.py:115
  388.3 65.6 %collective-permute-start.27 = (bf16[96,4096]{1,0:T(8,128)(2,1)}, bf16[96,4096]{1,0:T(8,128)(2,1)}, u32[]{:S(2)}, u32[]{:S(2)}) collective-permute-start(bf16[96,4096]{1,0:T(8,128)(2,1)} %get-tuple-element.340), channel_id=1, source_target_pairs={{0,6},{1,7},{2,0},{3,1},{4,2},{5,3},{6,4},{7,5},{8,14},{9,15},{10,... | collective-permute-start | bytes 2359304 | tf_op jit(solution)/shard_map/ppermute | solution.py:115
  468.6 212.8 %all-gather.15.cloned.1.call-start = ((), (), s32[]{:S(2)}) async-start(), calls=%async_computation.4 | async-start | bytes 14155776 | tf_op jit(solution)/shard_map/all_gather | solution.py:208
  484.5 38.7 %collective-permute-start.29 = (bf16[96,4096]{1,0:T(8,128)(2,1)}, bf16[96,4096]{1,0:T(8,128)(2,1)}, u32[]{:S(2)}, u32[]{:S(2)}) collective-permute-start(bf16[96,4096]{1,0:T(8,128)(2,1)} %get-tuple-element.335), channel_id=1, source_target_pairs={{0,2},{1,3},{2,4},{3,5},{4,6},{5,7},{6,0},{7,1},{8,10},{9,11},{10,... | collective-permute-start | bytes 2359304 | tf_op jit(solution)/shard_map/ppermute | solution.py:115
  484.5 38.7 %collective-permute-start.30 = (bf16[96,4096]{1,0:T(8,128)(2,1)}, bf16[96,4096]{1,0:T(8,128)(2,1)}, u32[]{:S(2)}, u32[]{:S(2)}) collective-permute-start(bf16[96,4096]{1,0:T(8,128)(2,1)} %get-tuple-element.334), channel_id=1, source_target_pairs={{0,6},{1,7},{2,0},{3,1},{4,2},{5,3},{6,4},{7,5},{8,14},{9,15},{10,... | collective-permute-start | bytes 2359304 | tf_op jit(solution)/shard_map/ppermute | solution.py:115
  487.7 92.0 %collective-permute-start.31 = (bf16[96,4096]{1,0:T(8,128)(2,1)}, bf16[96,4096]{1,0:T(8,128)(2,1)S(1)}, u32[]{:S(2)}, u32[]{:S(2)}) collective-permute-start(bf16[96,4096]{1,0:T(8,128)(2,1)} %get-tuple-element.333), channel_id=1, source_target_pairs={{0,6},{1,7},{2,0},{3,1},{4,2},{5,3},{6,4},{7,5},{8,14},{9,15},{10,... | collective-permute-start | bytes 2359304 | tf_op jit(solution)/shard_map/ppermute | solution.py:115
  487.8 92.0 %collective-permute-start.33 = (bf16[96,4096]{1,0:T(8,128)(2,1)}, bf16[96,4096]{1,0:T(8,128)(2,1)S(1)}, u32[]{:S(2)}, u32[]{:S(2)}) collective-permute-start(bf16[96,4096]{1,0:T(8,128)(2,1)} %get-tuple-element.332), channel_id=1, source_target_pairs={{0,2},{1,3},{2,4},{3,5},{4,6},{5,7},{6,0},{7,1},{8,10},{9,11},{10,... | collective-permute-start | bytes 2359304 | tf_op jit(solution)/shard_map/ppermute | solution.py:115
  526.5 63.2 %collective-permute-start.32 = (bf16[96,4096]{1,0:T(8,128)(2,1)S(1)}, bf16[96,4096]{1,0:T(8,128)(2,1)S(1)}, u32[]{:S(2)}, u32[]{:S(2)}) collective-permute-start(bf16[96,4096]{1,0:T(8,128)(2,1)S(1)} %get-tuple-element.331), channel_id=1, source_target_pairs={{0,2},{1,3},{2,4},{3,5},{4,6},{5,7},{6,0},{7,1},{8,10},{9,11},{10,... | collective-permute-start | bytes 2359304 | tf_op jit(solution)/shard_map/ppermute | solution.py:115
  526.6 63.1 %collective-permute-start.34 = (bf16[96,4096]{1,0:T(8,128)(2,1)S(1)}, bf16[96,4096]{1,0:T(8,128)(2,1)S(1)}, u32[]{:S(2)}, u32[]{:S(2)}) collective-permute-start(bf16[96,4096]{1,0:T(8,128)(2,1)S(1)} %get-tuple-element.330), channel_id=1, source_target_pairs={{0,6},{1,7},{2,0},{3,1},{4,2},{5,3},{6,4},{7,5},{8,14},{9,15},{10,... | collective-permute-start | bytes 2359304 | tf_op jit(solution)/shard_map/ppermute | solution.py:115
  596.6 197.5 %all-gather.17.cloned.1.call-start = ((), (), s32[]{:S(2)}) async-start(), calls=%async_computation.5 | async-start | bytes 14155776 | tf_op jit(solution)/shard_map/all_gather | solution.py:208
  650.8 62.3 %collective-permute-start.39 = (bf16[96,4096]{1,0:T(8,128)(2,1)S(1)}, bf16[96,4096]{1,0:T(8,128)(2,1)S(1)}, u32[]{:S(2)}, u32[]{:S(2)}) collective-permute-start(bf16[96,4096]{1,0:T(8,128)(2,1)S(1)} %get-tuple-element.325), channel_id=1, source_target_pairs={{0,6},{1,7},{2,0},{3,1},{4,2},{5,3},{6,4},{7,5},{8,14},{9,15},{10,... | collective-permute-start | bytes 2359304 | tf_op jit(solution)/shard_map/ppermute | solution.py:115
  651.7 61.4 %collective-permute-start.41 = (bf16[96,4096]{1,0:T(8,128)(2,1)S(1)}, bf16[96,4096]{1,0:T(8,128)(2,1)S(1)}, u32[]{:S(2)}, u32[]{:S(2)}) collective-permute-start(bf16[96,4096]{1,0:T(8,128)(2,1)S(1)} %get-tuple-element.324), channel_id=1, source_target_pairs={{0,2},{1,3},{2,4},{3,5},{4,6},{5,7},{6,0},{7,1},{8,10},{9,11},{10,... | collective-permute-start | bytes 2359304 | tf_op jit(solution)/shard_map/ppermute | solution.py:115
  678.2 34.9 %collective-permute-start.40 = (bf16[96,4096]{1,0:T(8,128)(2,1)}, bf16[96,4096]{1,0:T(8,128)(2,1)}, u32[]{:S(2)}, u32[]{:S(2)}) collective-permute-start(bf16[96,4096]{1,0:T(8,128)(2,1)} %get-tuple-element.323), channel_id=1, source_target_pairs={{0,2},{1,3},{2,4},{3,5},{4,6},{5,7},{6,0},{7,1},{8,10},{9,11},{10,... | collective-permute-start | bytes 2359304 | tf_op jit(solution)/shard_map/ppermute | solution.py:115
  679.4 33.7 %collective-permute-start.42 = (bf16[96,4096]{1,0:T(8,128)(2,1)}, bf16[96,4096]{1,0:T(8,128)(2,1)}, u32[]{:S(2)}, u32[]{:S(2)}) collective-permute-start(bf16[96,4096]{1,0:T(8,128)(2,1)} %get-tuple-element.322), channel_id=1, source_target_pairs={{0,6},{1,7},{2,0},{3,1},{4,2},{5,3},{6,4},{7,5},{8,14},{9,15},{10,... | collective-permute-start | bytes 2359304 | tf_op jit(solution)/shard_map/ppermute | solution.py:115
  719.8 67.4 %collective-permute-start.36 = (bf16[768,4096]{1,0:T(8,128)(2,1)}, bf16[768,4096]{1,0:T(8,128)(2,1)S(1)}, u32[]{:S(2)}, u32[]{:S(2)}) collective-permute-start(bf16[768,4096]{1,0:T(8,128)(2,1)} %convolution_convert_fusion.11), channel_id=1, source_target_pairs={{0,1},{1,0},{2,3},{3,2},{4,5},{5,4},{6,7},{7,6},{8,9},{9,8},{10,11... | collective-permute-start | bytes 18874376 | tf_op jit(solution)/shard_map/ppermute | solution.py:115
  769.3 56.6 %collective-permute-start.46 = (bf16[768,4096]{1,0:T(8,128)(2,1)}, bf16[768,4096]{1,0:T(8,128)(2,1)}, u32[]{:S(2)}, u32[]{:S(2)}) collective-permute-start(bf16[768,4096]{1,0:T(8,128)(2,1)} %convolution_convert_fusion.9), channel_id=1, source_target_pairs={{0,1},{1,0},{2,3},{3,2},{4,5},{5,4},{6,7},{7,6},{8,9},{9,8},{10,11... | collective-permute-start | bytes 18874376 | tf_op jit(solution)/shard_map/ppermute | solution.py:115
  790.8 40.2 %collective-permute-start.44 = (bf16[96,4096]{1,0:T(8,128)(2,1)}, bf16[96,4096]{1,0:T(8,128)(2,1)}, u32[]{:S(2)}, u32[]{:S(2)}) collective-permute-start(bf16[96,4096]{1,0:T(8,128)(2,1)} %get-tuple-element.319), channel_id=1, source_target_pairs={{0,2},{1,3},{2,4},{3,5},{4,6},{5,7},{6,0},{7,1},{8,10},{9,11},{10,... | collective-permute-start | bytes 2359304 | tf_op jit(solution)/shard_map/ppermute | solution.py:115
  790.8 40.2 %collective-permute-start.45 = (bf16[96,4096]{1,0:T(8,128)(2,1)}, bf16[96,4096]{1,0:T(8,128)(2,1)}, u32[]{:S(2)}, u32[]{:S(2)}) collective-permute-start(bf16[96,4096]{1,0:T(8,128)(2,1)} %get-tuple-element.318), channel_id=1, source_target_pairs={{0,6},{1,7},{2,0},{3,1},{4,2},{5,3},{6,4},{7,5},{8,14},{9,15},{10,... | collective-permute-start | bytes 2359304 | tf_op jit(solution)/shard_map/ppermute | solution.py:115
  885.1 63.3 %collective-permute-start.52 = (bf16[768,4096]{1,0:T(8,128)(2,1)}, bf16[768,4096]{1,0:T(8,128)(2,1)S(1)}, u32[]{:S(2)}, u32[]{:S(2)}) collective-permute-start(bf16[768,4096]{1,0:T(8,128)(2,1)} %convolution_convert_fusion.7), channel_id=1, source_target_pairs={{0,1},{1,0},{2,3},{3,2},{4,5},{5,4},{6,7},{7,6},{8,9},{9,8},{10,11... | collective-permute-start | bytes 18874376 | tf_op jit(solution)/shard_map/ppermute | solution.py:115
  888.5 44.2 %collective-permute-start.53 = (bf16[96,4096]{1,0:T(8,128)(2,1)}, bf16[96,4096]{1,0:T(8,128)(2,1)}, u32[]{:S(2)}, u32[]{:S(2)}) collective-permute-start(bf16[96,4096]{1,0:T(8,128)(2,1)} %get-tuple-element.312), channel_id=1, source_target_pairs={{0,6},{1,7},{2,0},{3,1},{4,2},{5,3},{6,4},{7,5},{8,14},{9,15},{10,... | collective-permute-start | bytes 2359304 | tf_op jit(solution)/shard_map/ppermute | solution.py:115
  888.5 46.1 %collective-permute-start.55 = (bf16[96,4096]{1,0:T(8,128)(2,1)}, bf16[96,4096]{1,0:T(8,128)(2,1)}, u32[]{:S(2)}, u32[]{:S(2)}) collective-permute-start(bf16[96,4096]{1,0:T(8,128)(2,1)} %get-tuple-element.313), channel_id=1, source_target_pairs={{0,2},{1,3},{2,4},{3,5},{4,6},{5,7},{6,0},{7,1},{8,10},{9,11},{10,... | collective-permute-start | bytes 2359304 | tf_op jit(solution)/shard_map/ppermute | solution.py:115
  940.9 33.6 %collective-permute-start.47 = (bf16[96,4096]{1,0:T(8,128)(2,1)}, bf16[96,4096]{1,0:T(8,128)(2,1)S(1)}, u32[]{:S(2)}, u32[]{:S(2)}) collective-permute-start(bf16[96,4096]{1,0:T(8,128)(2,1)} %get-tuple-element.311), channel_id=1, source_target_pairs={{0,2},{1,3},{2,4},{3,5},{4,6},{5,7},{6,0},{7,1},{8,10},{9,11},{10,... | collective-permute-start | bytes 2359304 | tf_op jit(solution)/shard_map/ppermute | solution.py:115
  940.9 33.6 %collective-permute-start.49 = (bf16[96,4096]{1,0:T(8,128)(2,1)}, bf16[96,4096]{1,0:T(8,128)(2,1)S(1)}, u32[]{:S(2)}, u32[]{:S(2)}) collective-permute-start(bf16[96,4096]{1,0:T(8,128)(2,1)} %get-tuple-element.310), channel_id=1, source_target_pairs={{0,6},{1,7},{2,0},{3,1},{4,2},{5,3},{6,4},{7,5},{8,14},{9,15},{10,... | collective-permute-start | bytes 2359304 | tf_op jit(solution)/shard_map/ppermute | solution.py:115
  950.6 40.7 %collective-permute-start.58 = (bf16[96,4096]{1,0:T(8,128)(2,1)}, bf16[96,4096]{1,0:T(8,128)(2,1)S(1)}, u32[]{:S(2)}, u32[]{:S(2)}) collective-permute-start(bf16[96,4096]{1,0:T(8,128)(2,1)} %get-tuple-element.307), channel_id=1, source_target_pairs={{0,2},{1,3},{2,4},{3,5},{4,6},{5,7},{6,0},{7,1},{8,10},{9,11},{10,... | collective-permute-start | bytes 2359304 | tf_op jit(solution)/shard_map/ppermute | solution.py:115
  957.0 34.4 %collective-permute-start.59 = (bf16[96,4096]{1,0:T(8,128)(2,1)}, bf16[96,4096]{1,0:T(8,128)(2,1)S(1)}, u32[]{:S(2)}, u32[]{:S(2)}) collective-permute-start(bf16[96,4096]{1,0:T(8,128)(2,1)} %get-tuple-element.306), channel_id=1, source_target_pairs={{0,6},{1,7},{2,0},{3,1},{4,2},{5,3},{6,4},{7,5},{8,14},{9,15},{10,... | collective-permute-start | bytes 2359304 | tf_op jit(solution)/shard_map/ppermute | solution.py:115
  960.7 46.9 %collective-permute-start.57 = (bf16[96,4096]{1,0:T(8,128)(2,1)S(1)}, bf16[96,4096]{1,0:T(8,128)(2,1)S(1)}, u32[]{:S(2)}, u32[]{:S(2)}) collective-permute-start(bf16[96,4096]{1,0:T(8,128)(2,1)S(1)} %get-tuple-element.305), channel_id=1, source_target_pairs={{0,6},{1,7},{2,0},{3,1},{4,2},{5,3},{6,4},{7,5},{8,14},{9,15},{10,... | collective-permute-start | bytes 2359304 | tf_op jit(solution)/shard_map/ppermute | solution.py:115
  974.5 33.7 %collective-permute-start.61 = (bf16[96,4096]{1,0:T(8,128)(2,1)S(1)}, bf16[96,4096]{1,0:T(8,128)(2,1)S(1)}, u32[]{:S(2)}, u32[]{:S(2)}) collective-permute-start(bf16[96,4096]{1,0:T(8,128)(2,1)S(1)} %get-tuple-element.304), channel_id=1, source_target_pairs={{0,2},{1,3},{2,4},{3,5},{4,6},{5,7},{6,0},{7,1},{8,10},{9,11},{10,... | collective-permute-start | bytes 2359304 | tf_op jit(solution)/shard_map/ppermute | solution.py:115
  (94 other events, 1883.1 us)
Sparse Core Ops, SparseCore 0:
  129.1 108.6 all-gather.6
  239.3 62.9 all-gather.8
  385.3 92.4 all-gather.10
  479.2 112.4 all-gather.12
  596.7 72.1 all-gather.14
  719.9 62.7 all-gather.16
where the time goes:
time: 1050 us; the launch traced here: 1040 us
  matrix products  368 us (35%)
  waiting for transfers between devices  283 us (27%)
  other arithmetic  126 us (12%)
  local copies, waits for them, and re-layouts  114 us (11%)
  starting transfers between devices  74 us (7%)
  Pallas kernels  58.1 us (6%)
  between operations  15.4 us (1%)
    ppermute x63, waiting for transfers between devices, shift(): return lax.ppermute(rows, 'tp', perm)  283 us
    dot_general x6, matrix products, project_down(): jnp.dot(rows, w_down, preferred_element_type=jnp.float32)  102 us
    dot_general x3, matrix products, activate(): up_proj = jnp.dot(rows, w_up, preferred_element_type=jnp.float32)  96 us
    dot_general x3, matrix products, row_steps(): jnp.dot(rows, w_gate, preferred_element_type=jnp.float32)  94.9 us
    gather x6, local copies, waits for them, and re-layouts, lookup(): embed_block.at[jnp.mod(ids - first_id, vocab_local)]  88.5 us
    ppermute x63, starting transfers between devices, shift(): return lax.ppermute(rows, 'tp', perm)  73.6 us
    pallas_call x3, Pallas kernels, local_attention(): pl.pallas_call(functools.partial(attention_body, 256), grid=(n_heads,), i...  58.1 us
    dot_general x3, matrix products, row_steps(): jnp.dot(rows, w_qkv, preferred_element_type=jnp.float32)  46.1 us
  transfers between devices with their start and end apart: 69, of which 25 were waited for; matrix products, arithmetic and copies ran while one was open for 46% of the time, Pallas kernels for 6%

commit v1 on v0

--- a/solution.py
+++ b/solution.py
@@ -83,6 +83,37 @@
     )(positions[None, :], positions[:, None], qkv, qkv, qkv, cos_tab, sin_tab)
 
 
+def gate_up_body(parity_ref, rows_ref, gate_ref, up_ref, out_ref):
+    rows = rows_ref[...].reshape(out_ref.shape[0], rows_ref.shape[-1])
+    gate = jnp.dot(rows, gate_ref[...], preferred_element_type=jnp.float32)
+    up_proj = jnp.dot(rows, up_ref[...], preferred_element_type=jnp.float32)
+    out_ref[...] = (jax.nn.gelu(gate, approximate=True) * up_proj).astype(jnp.bfloat16)
+
+
+def gate_up(rows, parity, w_gate, w_up, chunk):
+    seq_len, model_dim = rows.shape
+    width = w_gate.shape[1]
+    n_pair, col_tile = seq_len // (2 * chunk), 256
+    out_rows = n_pair * chunk
+    return pl.pallas_call(
+        gate_up_body,
+        grid_spec=pltpu.PrefetchScalarGridSpec(
+            num_scalar_prefetch=1,
+            grid=(width // col_tile,),
+            in_specs=[
+                pl.BlockSpec((n_pair, None, chunk, model_dim), lambda j, parity: (0, parity[0], 0, 0)),
+                pl.BlockSpec((model_dim, col_tile), lambda j, parity: (0, j)),
+                pl.BlockSpec((model_dim, col_tile), lambda j, parity: (0, j)),
+            ],
+            out_specs=pl.BlockSpec((out_rows, col_tile), lambda j, parity: (0, j)),
+        ),
+        out_shape=jax.ShapeDtypeStruct((out_rows, width), jnp.bfloat16),
+        compiler_params=pltpu.CompilerParams(vmem_limit_bytes=40 * 1024 * 1024),
+        cost_estimate=pl.CostEstimate(flops=4 * out_rows * model_dim * width, bytes_accessed=4 * model_dim * width, transcendentals=0),
+        name="gate_up",
+    )(parity.reshape(1).astype(jnp.int32), rows.reshape(n_pair, 2, chunk, model_dim), w_gate, w_up)
+
+
 def solution(mesh):
     in_specs = (P("dp", None), P("dp", None), P("tp", None), P(None, "tp", None), P(None, "tp", None), P(None, "tp", None), P("tp", None, None), P(None, "tp"), P(None, "tp"), P("tp", None), P(None), P(None), P(None), P(None))
     n_dev = mesh.shape["tp"]
@@ -206,19 +237,14 @@
 
             resid_one, normed = yield from ring_steps(own, from_partner, add_sums, after_attention)
             mlp_in = lax.all_gather(normed, "tp", axis=0, tiled=True)
-            gate_pre = step(lambda rows: jnp.dot(rows, w_gate, preferred_element_type=jnp.float32), mlp_in)
-            yield
-
-            def activate(rows, gate_pre):
-                up_proj = jnp.dot(rows, w_up, preferred_element_type=jnp.float32)
-                return (jax.nn.gelu(gate_pre, approximate=True) * up_proj).astype(jnp.bfloat16)
-
-            ffn_act = step(activate, mlp_in, gate_pre)
-            yield
-            other = step(lambda rows: project_down(by_parity(rows, 1 - core)), ffn_act)
+            other_act = step(lambda rows: gate_up(rows, 1 - core, w_gate, w_up, chunk), mlp_in)
+            yield
+            other = step(project_down, other_act)
             from_partner = shift(other, to_partner)
             yield
-            own = step(lambda rows: project_down(by_parity(rows, core)), ffn_act)
+            own_act = step(lambda rows: gate_up(rows, core, w_gate, w_up, chunk), mlp_in)
+            yield
+            own = step(project_down, own_act)
             yield
 
             def after_ffw(down_proj):

time: 1050 us -> 1010 us (0.962)
  matrix products: 368 us -> 171 us
  Pallas kernels: 58.1 us -> 232 us
    dot_general x6 -> x0, matrix products: 191 us -> none  [the longest x3 96 us: activate(): up_proj = jnp.dot(rows, w_up, preferred_element_type=jnp.float32)]
    pallas_call x0 -> x6, Pallas kernels: none -> 174 us  [gate_up(): pl.pallas_call(gate_up_body, grid_spec=pltpu.PrefetchScalarGridSpec(num_s...]
  transfers between devices with their start and end apart: 69 -> 69, of which waited for: 25 -> 26; matrix products, arithmetic and copies ran while one was open for 46% -> 33% of each run, Pallas kernels for 6% -> 23%
where the time goes in v1:
time: 1010 us; the launch traced here: 997 us
  waiting for transfers between devices  274 us (27%)
  Pallas kernels  232 us (23%)
  matrix products  171 us (17%)
  other arithmetic  123 us (12%)
  local copies, waits for them, and re-layouts  109 us (11%)
  starting transfers between devices  72.7 us (7%)
  between operations  15.5 us (2%)
    ppermute x63, waiting for transfers between devices, shift(): return lax.ppermute(rows, 'tp', perm)  274 us
    pallas_call x6, Pallas kernels, gate_up(): pl.pallas_call(gate_up_body, grid_spec=pltpu.PrefetchScalarGridSpec(num_s...  174 us
    dot_general x6, matrix products, project_down(): jnp.dot(rows, w_down, preferred_element_type=jnp.float32)  99.6 us
    gather x6, local copies, waits for them, and re-layouts, lookup(): embed_block.at[jnp.mod(ids - first_id, vocab_local)]  88.3 us
    ppermute x63, starting transfers between devices, shift(): return lax.ppermute(rows, 'tp', perm)  72.4 us
    pallas_call x3, Pallas kernels, local_attention(): pl.pallas_call(functools.partial(attention_body, 256), grid=(n_heads,), i...  57.9 us
    dot_general x3, matrix products, row_steps(): jnp.dot(rows, w_qkv, preferred_element_type=jnp.float32)  45.9 us
    another operation x9, other arithmetic  28.4 us
  transfers between devices with their start and end apart: 69, of which 26 were waited for; matrix products, arithmetic and copies ran while one was open for 33% of the time, Pallas kernels for 23%

profile of v1, /device:TPU:112, one launch (start us, length us, event | category | flops | bytes accessed | tf_op | source)
XLA Modules:
  0.0 997.3 jit_solution(6666622377034193656)
XLA Ops:
  7.7 14.5 %gather_fusion = bf16[768,4096]{1,0:T(8,128)(2,1)} fusion(bf16[4000,4096]{1,0:T(8,128)(2,1)} %param.16, s32[1024]{0:T(1024)S(1)} %pad_clamp_fusion.5), kind=kCustom, calls=%fused_computation | custom fusion | bytes 12585984 | tf_op jit(solution)/shard_map/gather | solution.py:192
  22.3 14.5 %gather_fusion.1 = bf16[768,4096]{1,0:T(8,128)(2,1)} fusion(bf16[4000,4096]{1,0:T(8,128)(2,1)} %param.16, s32[1024]{0:T(1024)S(1)} %pad_clamp_fusion.4), kind=kCustom, calls=%fused_computation.1 | custom fusion | bytes 12585984 | tf_op jit(solution)/shard_map/gather | solution.py:192
  37.2 4.6 select_select_fusion.8
  41.8 14.7 %gather_fusion.2 = bf16[768,4096]{1,0:T(8,128)(2,1)} fusion(bf16[4000,4096]{1,0:T(8,128)(2,1)} %param.16, s32[1024]{0:T(1024)S(1)} %pad_clamp_fusion.3), kind=kCustom, calls=%fused_computation.2 | custom fusion | bytes 12585984 | tf_op jit(solution)/shard_map/gather | solution.py:192
  63.4 16.0 %collective-permute-done.2 = bf16[96,4096]{1,0:T(8,128)(2,1)S(1)} collective-permute-done((bf16[96,4096]{1,0:T(8,128)(2,1)S(1)}, bf16[96,4096]{1,0:T(8,128)(2,1)S(1)}, u32[]{:S(2)}, u32[]{:S(2)}) %collective-permute-start.2) | collective-permute-done | bytes 786464 | tf_op jit(solution)/shard_map/ppermute | solution.py:146
  87.6 14.6 %gather_fusion.3 = bf16[768,4096]{1,0:T(8,128)(2,1)} fusion(bf16[4000,4096]{1,0:T(8,128)(2,1)} %param.16, s32[1024]{0:T(1024)S(1)} %pad_clamp_fusion.2), kind=kCustom, calls=%fused_computation.3 | custom fusion | bytes 12585984 | tf_op jit(solution)/shard_map/gather | solution.py:192
  102.2 4.6 select_select_fusion.4
  106.8 14.8 %gather_fusion.4 = bf16[768,4096]{1,0:T(8,128)(2,1)} fusion(bf16[4000,4096]{1,0:T(8,128)(2,1)} %param.16, s32[1024]{0:T(1024)S(1)} %pad_clamp_fusion.1), kind=kCustom, calls=%fused_computation.4 | custom fusion | bytes 12585984 | tf_op jit(solution)/shard_map/gather | solution.py:192
  134.7 15.2 %gather_fusion.5 = bf16[768,4096]{1,0:T(8,128)(2,1)} fusion(bf16[4000,4096]{1,0:T(8,128)(2,1)} %param.16, s32[1024]{0:T(1024)S(1)} %pad_clamp_fusion), kind=kCustom, calls=%fused_computation.5 | custom fusion | bytes 12585984 | tf_op jit(solution)/shard_map/gather | solution.py:192
  149.9 9.6 collective-permute-done.10
  159.5 5.0 collective-permute-done.9
  175.6 22.6 %collective-permute-done.12 = bf16[96,4096]{1,0:T(8,128)(2,1)} collective-permute-done((bf16[96,4096]{1,0:T(8,128)(2,1)S(1)}, bf16[96,4096]{1,0:T(8,128)(2,1)}, u32[]{:S(2)}, u32[]{:S(2)}) %collective-permute-start.12) | collective-permute-done | bytes 786464 | tf_op jit(solution)/shard_map/ppermute | solution.py:146
  198.2 32.7 %collective-permute-done.11 = bf16[96,4096]{1,0:T(8,128)(2,1)S(1)} collective-permute-done((bf16[96,4096]{1,0:T(8,128)(2,1)S(1)}, bf16[96,4096]{1,0:T(8,128)(2,1)S(1)}, u32[]{:S(2)}, u32[]{:S(2)}) %collective-permute-start.11) | collective-permute-done | bytes 786464 | tf_op jit(solution)/shard_map/ppermute | solution.py:146
  237.7 4.9 copy.20
  244.4 8.6 multiply_sine_fusion
  255.4 15.0 %fusion.52.q_ref.k_ref.v_ref = f32[1536,768]{1,0:T(8,128)S(1)} fusion(bf16[1536,4096]{1,0:T(8,128)(2,1)} %all-gather.7.cloned.1.call-done, bf16[4096,128]{1,0:T(8,128)(2,1)} %bitcast.140, bf16[4096,128]{1,0:T(8,128)(2,1)} %bitcast.143, bf16[4096,512]{1,0:T(8,128)(2,1)} %bitcast.119), kind=kOutput, calls=%fused_computation.305 | convolution fusion | flops 9682550784 | bytes 23592960 | tf_op jit(solution)/shard_map/dot_general | solution.py:224
  270.5 19.5 %attention.3 = bf16[1536,512]{1,0:T(8,128)(2,1)S(1)} custom-call(s32[1,1536]{1,0:T(1,128)S(1)} %get-tuple-element.374.pos_row_ref, s32[1536,1]{1,0:T(8,128)S(1)} %copy-done.3, f32[1536,768]{1,0:T(8,128)S(1)} %fusion.52.q_ref.k_ref.v_ref, f32[1536,768]{1,0:T(8,128)S(1)} %fusion.52.q_ref.k_ref.v_ref, f32[1536,768]{1,0:T(8,128)S(1)} %fusion.52.q_ref.k_ref.v_ref, ...), custom_call_target="tpu_custom_call" | custom-call | flops 4831838208 | bytes 9437184 | tf_op jit(solution)/shard_map/attention/pallas_call | solution.py:66
  297.6 7.5 collective-permute-done.15
  313.4 14.5 %collective-permute-done.17 = bf16[96,4096]{1,0:T(8,128)(2,1)S(1)} collective-permute-done((bf16[96,4096]{1,0:T(8,128)(2,1)S(1)}, bf16[96,4096]{1,0:T(8,128)(2,1)S(1)}, u32[]{:S(2)}, u32[]{:S(2)}) %collective-permute-start.17) | collective-permute-done | bytes 786464 | tf_op jit(solution)/shard_map/ppermute | solution.py:146
  329.9 14.9 %collective-permute-done.22 = bf16[96,4096]{1,0:T(8,128)(2,1)S(1)} collective-permute-done((bf16[96,4096]{1,0:T(8,128)(2,1)S(1)}, bf16[96,4096]{1,0:T(8,128)(2,1)S(1)}, u32[]{:S(2)}, u32[]{:S(2)}) %collective-permute-start.22) | collective-permute-done | bytes 786464 | tf_op jit(solution)/shard_map/ppermute | solution.py:146
  348.9 16.2 %fusion.51.q_ref.k_ref.v_ref = f32[1536,768]{1,0:T(8,128)} fusion(bf16[1536,4096]{1,0:T(8,128)(2,1)} %all-gather.9.cloned.1.call-done, bf16[4096,128]{1,0:T(8,128)(2,1)} %bitcast.141, bf16[4096,128]{1,0:T(8,128)(2,1)} %bitcast.144, bf16[4096,512]{1,0:T(8,128)(2,1)} %bitcast.120), kind=kOutput, calls=%fused_computation.304 | convolution fusion | flops 9682550784 | bytes 23592960 | tf_op jit(solution)/shard_map/dot_general | solution.py:224
  365.2 12.6 %collective-permute-done.19 = bf16[96,4096]{1,0:T(8,128)(2,1)} collective-permute-done((bf16[96,4096]{1,0:T(8,128)(2,1)}, bf16[96,4096]{1,0:T(8,128)(2,1)}, u32[]{:S(2)}, u32[]{:S(2)}) %collective-permute-start.19) | collective-permute-done | bytes 786464 | tf_op jit(solution)/shard_map/ppermute | solution.py:146
  398.7 19.3 %attention.4 = bf16[1536,512]{1,0:T(8,128)(2,1)S(1)} custom-call(s32[1,1536]{1,0:T(1,128)S(1)} %get-tuple-element.376.pos_row_ref, s32[1536,1]{1,0:T(8,128)S(1)} %copy-done.4, f32[1536,768]{1,0:T(8,128)S(1)} %copy-done, f32[1536,768]{1,0:T(8,128)S(1)} %copy-done, f32[1536,768]{1,0:T(8,128)S(1)} %copy-done, f32[1536,128]{1,0:T(8,128)S(1)} %copy-done.2, ...), custom_call_target="tpu_custom_call" | custom-call | flops 4831838208 | bytes 9437184 | tf_op jit(solution)/shard_map/attention/pallas_call | solution.py:66
  422.0 31.5 %collective-permute-done.25 = bf16[96,4096]{1,0:T(8,128)(2,1)} collective-permute-done((bf16[96,4096]{1,0:T(8,128)(2,1)}, bf16[96,4096]{1,0:T(8,128)(2,1)}, u32[]{:S(2)}, u32[]{:S(2)}) %collective-permute-start.25) | collective-permute-done | bytes 786464 | tf_op jit(solution)/shard_map/ppermute | solution.py:146
  460.8 6.5 convolution_convert_fusion.3
  471.2 7.5 collective-permute-done.28
  487.6 29.1 %gate_up.6 = bf16[768,1792]{1,0:T(8,128)(2,1)S(1)} custom-call(s32[1]{0:T(128)} %bitcast.15.parity_ref, bf16[4,2,192,4096]{3,2,1,0:T(8,128)(2,1)} %bitcast.130, bf16[4096,1792]{1,0:T(8,128)(2,1)} %gate_ref.11, bf16[4096,1792]{1,0:T(8,128)(2,1)} %up_ref.11), custom_call_target="tpu_custom_call" | custom-call | flops 22548578304 | bytes 29360128 | tf_op jit(solution)/shard_map/gate_up/pallas_call | solution.py:98
  526.7 16.5 %convolution_convert_fusion.11 = bf16[768,4096]{1,0:T(8,128)(2,1)} fusion(bf16[768,1792]{1,0:T(8,128)(2,1)S(1)} %gate_up.6, bf16[1792,4096]{1,0:T(8,128)(2,1)} %param.23), kind=kOutput, calls=%fused_computation.17 | convolution fusion | flops 11277434880 | bytes 23724032 | tf_op jit(solution)/shard_map/dot_general | solution.py:202
  543.2 29.0 %gate_up.7 = bf16[768,1792]{1,0:T(8,128)(2,1)S(1)} custom-call(s32[1]{0:T(128)} %bitcast.14.parity_ref, bf16[4,2,192,4096]{3,2,1,0:T(8,128)(2,1)} %bitcast.131, bf16[4096,1792]{1,0:T(8,128)(2,1)} %gate_ref.11, bf16[4096,1792]{1,0:T(8,128)(2,1)} %up_ref.11), custom_call_target="tpu_custom_call" | custom-call | flops 22548578304 | bytes 29360128 | tf_op jit(solution)/shard_map/gate_up/pallas_call | solution.py:98
  572.3 13.4 %collective-permute-done.32 = bf16[96,4096]{1,0:T(8,128)(2,1)S(1)} collective-permute-done((bf16[96,4096]{1,0:T(8,128)(2,1)S(1)}, bf16[96,4096]{1,0:T(8,128)(2,1)S(1)}, u32[]{:S(2)}, u32[]{:S(2)}) %collective-permute-start.32) | collective-permute-done | bytes 786464 | tf_op jit(solution)/shard_map/ppermute | solution.py:146
  591.5 14.7 %fusion.50.q_ref.k_ref.v_ref = f32[1536,768]{1,0:T(8,128)S(1)} fusion(bf16[1536,4096]{1,0:T(8,128)(2,1)} %all-gather.13.cloned.1.call-done, bf16[4096,128]{1,0:T(8,128)(2,1)} %bitcast.142, bf16[4096,128]{1,0:T(8,128)(2,1)} %bitcast.145, bf16[4096,512]{1,0:T(8,128)(2,1)} %bitcast.121), kind=kOutput, calls=%fused_computation.303 | convolution fusion | flops 9682550784 | bytes 23592960 | tf_op jit(solution)/shard_map/dot_general | solution.py:224
  606.2 19.1 %attention.5 = bf16[1536,512]{1,0:T(8,128)(2,1)S(1)} custom-call(s32[1,1536]{1,0:T(1,128)S(1)} %get-tuple-element.375.pos_row_ref, s32[1536,1]{1,0:T(8,128)S(1)} %copy.17.pos_col_ref, f32[1536,768]{1,0:T(8,128)S(1)} %fusion.50.q_ref.k_ref.v_ref, f32[1536,768]{1,0:T(8,128)S(1)} %fusion.50.q_ref.k_ref.v_ref, f32[1536,768]{1,0:T(8,128)S(1)} %fusion.50.q_ref.k_ref.v_ref, ...), custom_call_target="tpu_custom_call" | custom-call | flops 4831838208 | bytes 9437184 | tf_op jit(solution)/shard_map/attention/pallas_call | solution.py:66
  633.3 7.7 collective-permute-done.35
  649.1 16.6 %convolution_convert_fusion.10 = bf16[768,4096]{1,0:T(8,128)(2,1)} fusion(bf16[768,1792]{1,0:T(8,128)(2,1)S(1)} %copy-done.6, bf16[1792,4096]{1,0:T(8,128)(2,1)} %param.23), kind=kOutput, calls=%fused_computation.16 | convolution fusion | flops 11277434880 | bytes 23724032 | tf_op jit(solution)/shard_map/dot_general | solution.py:202
  665.6 7.0 collective-permute-done.37
  677.8 28.8 %gate_up.8 = bf16[768,1792]{1,0:T(8,128)(2,1)S(1)} custom-call(s32[1]{0:T(128)} %bitcast.15.parity_ref, bf16[4,2,192,4096]{3,2,1,0:T(8,128)(2,1)} %bitcast.128, bf16[4096,1792]{1,0:T(8,128)(2,1)} %gate_ref.11, bf16[4096,1792]{1,0:T(8,128)(2,1)} %up_ref.11), custom_call_target="tpu_custom_call" | custom-call | flops 22548578304 | bytes 29360128 | tf_op jit(solution)/shard_map/gate_up/pallas_call | solution.py:98
  713.8 16.8 %convolution_convert_fusion.9 = bf16[768,4096]{1,0:T(8,128)(2,1)} fusion(bf16[768,1792]{1,0:T(8,128)(2,1)S(1)} %gate_up.8, bf16[1792,4096]{1,0:T(8,128)(2,1)} %param.23), kind=kOutput, calls=%fused_computation.15 | convolution fusion | flops 11277434880 | bytes 23724032 | tf_op jit(solution)/shard_map/dot_general | solution.py:202
  731.0 29.2 %gate_up.9 = bf16[768,1792]{1,0:T(8,128)(2,1)S(1)} custom-call(s32[1]{0:T(128)} %bitcast.14.parity_ref, bf16[4,2,192,4096]{3,2,1,0:T(8,128)(2,1)} %bitcast.129, bf16[4096,1792]{1,0:T(8,128)(2,1)} %gate_ref.11, bf16[4096,1792]{1,0:T(8,128)(2,1)} %up_ref.11), custom_call_target="tpu_custom_call" | custom-call | flops 22548578304 | bytes 29360128 | tf_op jit(solution)/shard_map/gate_up/pallas_call | solution.py:98
  760.2 16.6 %convolution_convert_fusion.8 = bf16[768,4096]{1,0:T(8,128)(2,1)} fusion(bf16[768,1792]{1,0:T(8,128)(2,1)S(1)} %gate_up.9, bf16[1792,4096]{1,0:T(8,128)(2,1)} %param.23), kind=kOutput, calls=%fused_computation.14 | convolution fusion | flops 11277434880 | bytes 23724032 | tf_op jit(solution)/shard_map/dot_general | solution.py:202
  783.6 29.2 %gate_up.10 = bf16[768,1792]{1,0:T(8,128)(2,1)S(1)} custom-call(s32[1]{0:T(128)} %bitcast.15.parity_ref, bf16[4,2,192,4096]{3,2,1,0:T(8,128)(2,1)} %bitcast.132, bf16[4096,1792]{1,0:T(8,128)(2,1)} %gate_ref.11, bf16[4096,1792]{1,0:T(8,128)(2,1)} %up_ref.11), custom_call_target="tpu_custom_call" | custom-call | flops 22548578304 | bytes 29360128 | tf_op jit(solution)/shard_map/gate_up/pallas_call | solution.py:98
  825.7 16.5 %convolution_convert_fusion.7 = bf16[768,4096]{1,0:T(8,128)(2,1)} fusion(bf16[768,1792]{1,0:T(8,128)(2,1)S(1)} %gate_up.10, bf16[1792,4096]{1,0:T(8,128)(2,1)} %param.23), kind=kOutput, calls=%fused_computation.13 | convolution fusion | flops 11277434880 | bytes 23724032 | tf_op jit(solution)/shard_map/dot_general | solution.py:202
  842.2 28.8 %gate_up.11 = bf16[768,1792]{1,0:T(8,128)(2,1)S(1)} custom-call(s32[1]{0:T(128)} %bitcast.14.parity_ref, bf16[4,2,192,4096]{3,2,1,0:T(8,128)(2,1)} %bitcast.133, bf16[4096,1792]{1,0:T(8,128)(2,1)} %gate_ref.11, bf16[4096,1792]{1,0:T(8,128)(2,1)} %up_ref.11), custom_call_target="tpu_custom_call" | custom-call | flops 22548578304 | bytes 29360128 | tf_op jit(solution)/shard_map/gate_up/pallas_call | solution.py:98
  878.6 16.7 %convolution_convert_fusion.6 = bf16[768,4096]{1,0:T(8,128)(2,1)} fusion(bf16[768,1792]{1,0:T(8,128)(2,1)S(1)} %gate_up.11, bf16[1792,4096]{1,0:T(8,128)(2,1)} %param.23), kind=kOutput, calls=%fused_computation.12 | convolution fusion | flops 11277434880 | bytes 23724032 | tf_op jit(solution)/shard_map/dot_general | solution.py:202
  907.2 8.5 collective-permute-done.43
  917.0 16.8 %collective-permute-done.47 = bf16[96,4096]{1,0:T(8,128)(2,1)S(1)} collective-permute-done((bf16[96,4096]{1,0:T(8,128)(2,1)}, bf16[96,4096]{1,0:T(8,128)(2,1)S(1)}, u32[]{:S(2)}, u32[]{:S(2)}) %collective-permute-start.47) | collective-permute-done | bytes 786464 | tf_op jit(solution)/shard_map/ppermute | solution.py:146
  936.1 14.6 %collective-permute-done.58 = bf16[96,4096]{1,0:T(8,128)(2,1)S(1)} collective-permute-done((bf16[96,4096]{1,0:T(8,128)(2,1)}, bf16[96,4096]{1,0:T(8,128)(2,1)S(1)}, u32[]{:S(2)}, u32[]{:S(2)}) %collective-permute-start.58) | collective-permute-done | bytes 786464 | tf_op jit(solution)/shard_map/ppermute | solution.py:146
  956.3 5.5 add_convert_fusion.4
  967.6 15.9 %collective-permute-done.60 = bf16[96,4096]{1,0:T(8,128)(2,1)S(1)} collective-permute-done((bf16[96,4096]{1,0:T(8,128)(2,1)S(1)}, bf16[96,4096]{1,0:T(8,128)(2,1)S(1)}, u32[]{:S(2)}, u32[]{:S(2)}) %collective-permute-start.60) | collective-permute-done | bytes 786464 | tf_op jit(solution)/shard_map/ppermute | solution.py:146
  (391 shorter events, 222.8 us)
Async XLA Ops:
  6.5 248.9 %all-gather.7.cloned.1.call-start = ((), (), s32[]{:S(2)}) async-start(), calls=%async_computation | async-start | bytes 14155776 | tf_op jit(solution)/shard_map/all_gather | solution.py:223
  56.5 45.7 %collective-permute-start.7 = (bf16[768,4096]{1,0:T(8,128)(2,1)}, bf16[768,4096]{1,0:T(8,128)(2,1)}, u32[]{:S(2)}, u32[]{:S(2)}) collective-permute-start(bf16[768,4096]{1,0:T(8,128)(2,1)} %gather_fusion.2), channel_id=1, source_target_pairs={{0,1},{1,0},{2,3},{3,2},{4,5},{5,4},{6,7},{7,6},{8,9},{9,8},{10,11... | collective-permute-start | bytes 18874376 | tf_op jit(solution)/shard_map/ppermute | solution.py:146
  61.3 60.4 %collective-permute-start.1 = (bf16[96,4096]{1,0:T(8,128)(2,1)}, bf16[96,4096]{1,0:T(8,128)(2,1)}, u32[]{:S(2)}, u32[]{:S(2)}) collective-permute-start(bf16[96,4096]{1,0:T(8,128)(2,1)} %get-tuple-element.359), channel_id=1, source_target_pairs={{0,6},{1,7},{2,0},{3,1},{4,2},{5,3},{6,4},{7,5},{8,14},{9,15},{10,... | collective-permute-start | bytes 2359304 | tf_op jit(solution)/shard_map/ppermute | solution.py:146
  63.4 58.3 %collective-permute-start.5 = (bf16[96,4096]{1,0:T(8,128)(2,1)S(1)}, bf16[96,4096]{1,0:T(8,128)(2,1)}, u32[]{:S(2)}, u32[]{:S(2)}) collective-permute-start(bf16[96,4096]{1,0:T(8,128)(2,1)S(1)} %get-tuple-element.356), channel_id=1, source_target_pairs={{0,2},{1,3},{2,4},{3,5},{4,6},{5,7},{6,0},{7,1},{8,10},{9,11},{10,... | collective-permute-start | bytes 2359304 | tf_op jit(solution)/shard_map/ppermute | solution.py:146
  84.3 37.4 %collective-permute-start.4 = (bf16[96,4096]{1,0:T(8,128)(2,1)}, bf16[96,4096]{1,0:T(8,128)(2,1)}, u32[]{:S(2)}, u32[]{:S(2)}) collective-permute-start(bf16[96,4096]{1,0:T(8,128)(2,1)} %get-tuple-element.355), channel_id=1, source_target_pairs={{0,2},{1,3},{2,4},{3,5},{4,6},{5,7},{6,0},{7,1},{8,10},{9,11},{10,... | collective-permute-start | bytes 2359304 | tf_op jit(solution)/shard_map/ppermute | solution.py:146
  85.9 35.8 %collective-permute-start.6 = (bf16[96,4096]{1,0:T(8,128)(2,1)}, bf16[96,4096]{1,0:T(8,128)(2,1)}, u32[]{:S(2)}, u32[]{:S(2)}) collective-permute-start(bf16[96,4096]{1,0:T(8,128)(2,1)} %get-tuple-element.354), channel_id=1, source_target_pairs={{0,6},{1,7},{2,0},{3,1},{4,2},{5,3},{6,4},{7,5},{8,14},{9,15},{10,... | collective-permute-start | bytes 2359304 | tf_op jit(solution)/shard_map/ppermute | solution.py:146
  128.8 220.0 %all-gather.9.cloned.1.call-start = ((), (), s32[]{:S(2)}) async-start(), calls=%async_computation.1 | async-start | bytes 14155776 | tf_op jit(solution)/shard_map/all_gather | solution.py:223
  128.9 42.7 %collective-permute-start.14 = (bf16[768,4096]{1,0:T(8,128)(2,1)}, bf16[768,4096]{1,0:T(8,128)(2,1)}, u32[]{:S(2)}, u32[]{:S(2)}) collective-permute-start(bf16[768,4096]{1,0:T(8,128)(2,1)} %gather_fusion.4), channel_id=1, source_target_pairs={{0,1},{1,0},{2,3},{3,2},{4,5},{5,4},{6,7},{7,6},{8,9},{9,8},{10,11... | collective-permute-start | bytes 18874376 | tf_op jit(solution)/shard_map/ppermute | solution.py:146
  130.6 34.0 %collective-permute-start.9 = (bf16[96,4096]{1,0:T(8,128)(2,1)S(1)}, bf16[96,4096]{1,0:T(8,128)(2,1)}, u32[]{:S(2)}, u32[]{:S(2)}) collective-permute-start(bf16[96,4096]{1,0:T(8,128)(2,1)S(1)} %get-tuple-element.353), channel_id=1, source_target_pairs={{0,2},{1,3},{2,4},{3,5},{4,6},{5,7},{6,0},{7,1},{8,10},{9,11},{10,... | collective-permute-start | bytes 2359304 | tf_op jit(solution)/shard_map/ppermute | solution.py:146
  131.3 66.9 %collective-permute-start.12 = (bf16[96,4096]{1,0:T(8,128)(2,1)S(1)}, bf16[96,4096]{1,0:T(8,128)(2,1)}, u32[]{:S(2)}, u32[]{:S(2)}) collective-permute-start(bf16[96,4096]{1,0:T(8,128)(2,1)S(1)} %get-tuple-element.351), channel_id=1, source_target_pairs={{0,2},{1,3},{2,4},{3,5},{4,6},{5,7},{6,0},{7,1},{8,10},{9,11},{10,... | collective-permute-start | bytes 2359304 | tf_op jit(solution)/shard_map/ppermute | solution.py:146
  131.7 66.5 %collective-permute-start.8 = (bf16[96,4096]{1,0:T(8,128)(2,1)S(1)}, bf16[96,4096]{1,0:T(8,128)(2,1)}, u32[]{:S(2)}, u32[]{:S(2)}) collective-permute-start(bf16[96,4096]{1,0:T(8,128)(2,1)S(1)} %get-tuple-element.350), channel_id=1, source_target_pairs={{0,6},{1,7},{2,0},{3,1},{4,2},{5,3},{6,4},{7,5},{8,14},{9,15},{10,... | collective-permute-start | bytes 2359304 | tf_op jit(solution)/shard_map/ppermute | solution.py:146
  168.3 62.7 %collective-permute-start.11 = (bf16[96,4096]{1,0:T(8,128)(2,1)S(1)}, bf16[96,4096]{1,0:T(8,128)(2,1)S(1)}, u32[]{:S(2)}, u32[]{:S(2)}) collective-permute-start(bf16[96,4096]{1,0:T(8,128)(2,1)S(1)} %get-tuple-element.347), channel_id=1, source_target_pairs={{0,2},{1,3},{2,4},{3,5},{4,6},{5,7},{6,0},{7,1},{8,10},{9,11},{10,... | collective-permute-start | bytes 2359304 | tf_op jit(solution)/shard_map/ppermute | solution.py:146
  168.4 62.6 %collective-permute-start.13 = (bf16[96,4096]{1,0:T(8,128)(2,1)S(1)}, bf16[96,4096]{1,0:T(8,128)(2,1)S(1)}, u32[]{:S(2)}, u32[]{:S(2)}) collective-permute-start(bf16[96,4096]{1,0:T(8,128)(2,1)S(1)} %get-tuple-element.346), channel_id=1, source_target_pairs={{0,6},{1,7},{2,0},{3,1},{4,2},{5,3},{6,4},{7,5},{8,14},{9,15},{10,... | collective-permute-start | bytes 2359304 | tf_op jit(solution)/shard_map/ppermute | solution.py:146
  237.6 249.9 %all-gather.11.cloned.1.call-start = ((), (), s32[]{:S(2)}) async-start(), calls=%async_computation.2 | async-start | bytes 14155776 | tf_op jit(solution)/shard_map/all_gather | solution.py:239
  310.2 34.6 %collective-permute-start.22 = (bf16[96,4096]{1,0:T(8,128)(2,1)S(1)}, bf16[96,4096]{1,0:T(8,128)(2,1)S(1)}, u32[]{:S(2)}, u32[]{:S(2)}) collective-permute-start(bf16[96,4096]{1,0:T(8,128)(2,1)S(1)} %copy-done.51), channel_id=1, source_target_pairs={{0,2},{1,3},{2,4},{3,5},{4,6},{5,7},{6,0},{7,1},{8,10},{9,11},{10,... | collective-permute-start | bytes 2359304 | tf_op jit(solution)/shard_map/ppermute | solution.py:146
  310.2 34.6 %collective-permute-start.23 = (bf16[96,4096]{1,0:T(8,128)(2,1)S(1)}, bf16[96,4096]{1,0:T(8,128)(2,1)S(1)}, u32[]{:S(2)}, u32[]{:S(2)}) collective-permute-start(bf16[96,4096]{1,0:T(8,128)(2,1)S(1)} %copy-done.50), channel_id=1, source_target_pairs={{0,6},{1,7},{2,0},{3,1},{4,2},{5,3},{6,4},{7,5},{8,14},{9,15},{10,... | collective-permute-start | bytes 2359304 | tf_op jit(solution)/shard_map/ppermute | solution.py:146
  313.4 51.7 %collective-permute-start.16 = (bf16[96,4096]{1,0:T(8,128)(2,1)S(1)}, bf16[96,4096]{1,0:T(8,128)(2,1)}, u32[]{:S(2)}, u32[]{:S(2)}) collective-permute-start(bf16[96,4096]{1,0:T(8,128)(2,1)S(1)} %get-tuple-element.336), channel_id=1, source_target_pairs={{0,6},{1,7},{2,0},{3,1},{4,2},{5,3},{6,4},{7,5},{8,14},{9,15},{10,... | collective-permute-start | bytes 2359304 | tf_op jit(solution)/shard_map/ppermute | solution.py:146
  327.9 37.2 %collective-permute-start.20 = (bf16[96,4096]{1,0:T(8,128)(2,1)S(1)}, bf16[96,4096]{1,0:T(8,128)(2,1)}, u32[]{:S(2)}, u32[]{:S(2)}) collective-permute-start(bf16[96,4096]{1,0:T(8,128)(2,1)S(1)} %get-tuple-element.337), channel_id=1, source_target_pairs={{0,2},{1,3},{2,4},{3,5},{4,6},{5,7},{6,0},{7,1},{8,10},{9,11},{10,... | collective-permute-start | bytes 2359304 | tf_op jit(solution)/shard_map/ppermute | solution.py:146
  329.9 47.9 %collective-permute-start.19 = (bf16[96,4096]{1,0:T(8,128)(2,1)}, bf16[96,4096]{1,0:T(8,128)(2,1)}, u32[]{:S(2)}, u32[]{:S(2)}) collective-permute-start(bf16[96,4096]{1,0:T(8,128)(2,1)} %get-tuple-element.335), channel_id=1, source_target_pairs={{0,2},{1,3},{2,4},{3,5},{4,6},{5,7},{6,0},{7,1},{8,10},{9,11},{10,... | collective-permute-start | bytes 2359304 | tf_op jit(solution)/shard_map/ppermute | solution.py:146
  384.8 206.7 %all-gather.13.cloned.1.call-start = ((), (), s32[]{:S(2)}) async-start(), calls=%async_computation.3 | async-start | bytes 14155776 | tf_op jit(solution)/shard_map/all_gather | solution.py:223
  387.9 34.1 %collective-permute-start.26 = (bf16[96,4096]{1,0:T(8,128)(2,1)}, bf16[96,4096]{1,0:T(8,128)(2,1)}, u32[]{:S(2)}, u32[]{:S(2)}) collective-permute-start(bf16[96,4096]{1,0:T(8,128)(2,1)} %get-tuple-element.342), channel_id=1, source_target_pairs={{0,2},{1,3},{2,4},{3,5},{4,6},{5,7},{6,0},{7,1},{8,10},{9,11},{10,... | collective-permute-start | bytes 2359304 | tf_op jit(solution)/shard_map/ppermute | solution.py:146
  387.9 65.5 %collective-permute-start.25 = (bf16[96,4096]{1,0:T(8,128)(2,1)}, bf16[96,4096]{1,0:T(8,128)(2,1)}, u32[]{:S(2)}, u32[]{:S(2)}) collective-permute-start(bf16[96,4096]{1,0:T(8,128)(2,1)} %get-tuple-element.333), channel_id=1, source_target_pairs={{0,2},{1,3},{2,4},{3,5},{4,6},{5,7},{6,0},{7,1},{8,10},{9,11},{10,... | collective-permute-start | bytes 2359304 | tf_op jit(solution)/shard_map/ppermute | solution.py:146
  387.9 65.5 %collective-permute-start.27 = (bf16[96,4096]{1,0:T(8,128)(2,1)}, bf16[96,4096]{1,0:T(8,128)(2,1)}, u32[]{:S(2)}, u32[]{:S(2)}) collective-permute-start(bf16[96,4096]{1,0:T(8,128)(2,1)} %get-tuple-element.332), channel_id=1, source_target_pairs={{0,6},{1,7},{2,0},{3,1},{4,2},{5,3},{6,4},{7,5},{8,14},{9,15},{10,... | collective-permute-start | bytes 2359304 | tf_op jit(solution)/shard_map/ppermute | solution.py:146
  460.7 217.1 %all-gather.15.cloned.1.call-start = ((), (), s32[]{:S(2)}) async-start(), calls=%async_computation.4 | async-start | bytes 14155776 | tf_op jit(solution)/shard_map/all_gather | solution.py:239
  482.3 36.9 %collective-permute-start.29 = (bf16[96,4096]{1,0:T(8,128)(2,1)}, bf16[96,4096]{1,0:T(8,128)(2,1)}, u32[]{:S(2)}, u32[]{:S(2)}) collective-permute-start(bf16[96,4096]{1,0:T(8,128)(2,1)} %get-tuple-element.327), channel_id=1, source_target_pairs={{0,2},{1,3},{2,4},{3,5},{4,6},{5,7},{6,0},{7,1},{8,10},{9,11},{10,... | collective-permute-start | bytes 2359304 | tf_op jit(solution)/shard_map/ppermute | solution.py:146
  482.3 38.2 %collective-permute-start.30 = (bf16[96,4096]{1,0:T(8,128)(2,1)}, bf16[96,4096]{1,0:T(8,128)(2,1)}, u32[]{:S(2)}, u32[]{:S(2)}) collective-permute-start(bf16[96,4096]{1,0:T(8,128)(2,1)} %get-tuple-element.326), channel_id=1, source_target_pairs={{0,6},{1,7},{2,0},{3,1},{4,2},{5,3},{6,4},{7,5},{8,14},{9,15},{10,... | collective-permute-start | bytes 2359304 | tf_op jit(solution)/shard_map/ppermute | solution.py:146
  485.5 86.7 %collective-permute-start.31 = (bf16[96,4096]{1,0:T(8,128)(2,1)}, bf16[96,4096]{1,0:T(8,128)(2,1)S(1)}, u32[]{:S(2)}, u32[]{:S(2)}) collective-permute-start(bf16[96,4096]{1,0:T(8,128)(2,1)} %get-tuple-element.325), channel_id=1, source_target_pairs={{0,6},{1,7},{2,0},{3,1},{4,2},{5,3},{6,4},{7,5},{8,14},{9,15},{10,... | collective-permute-start | bytes 2359304 | tf_op jit(solution)/shard_map/ppermute | solution.py:146
  485.6 86.7 %collective-permute-start.33 = (bf16[96,4096]{1,0:T(8,128)(2,1)}, bf16[96,4096]{1,0:T(8,128)(2,1)S(1)}, u32[]{:S(2)}, u32[]{:S(2)}) collective-permute-start(bf16[96,4096]{1,0:T(8,128)(2,1)} %get-tuple-element.324), channel_id=1, source_target_pairs={{0,2},{1,3},{2,4},{3,5},{4,6},{5,7},{6,0},{7,1},{8,10},{9,11},{10,... | collective-permute-start | bytes 2359304 | tf_op jit(solution)/shard_map/ppermute | solution.py:146
  522.7 63.0 %collective-permute-start.32 = (bf16[96,4096]{1,0:T(8,128)(2,1)S(1)}, bf16[96,4096]{1,0:T(8,128)(2,1)S(1)}, u32[]{:S(2)}, u32[]{:S(2)}) collective-permute-start(bf16[96,4096]{1,0:T(8,128)(2,1)S(1)} %get-tuple-element.323), channel_id=1, source_target_pairs={{0,2},{1,3},{2,4},{3,5},{4,6},{5,7},{6,0},{7,1},{8,10},{9,11},{10,... | collective-permute-start | bytes 2359304 | tf_op jit(solution)/shard_map/ppermute | solution.py:146
  522.8 64.1 %collective-permute-start.34 = (bf16[96,4096]{1,0:T(8,128)(2,1)S(1)}, bf16[96,4096]{1,0:T(8,128)(2,1)S(1)}, u32[]{:S(2)}, u32[]{:S(2)}) collective-permute-start(bf16[96,4096]{1,0:T(8,128)(2,1)S(1)} %get-tuple-element.322), channel_id=1, source_target_pairs={{0,6},{1,7},{2,0},{3,1},{4,2},{5,3},{6,4},{7,5},{8,14},{9,15},{10,... | collective-permute-start | bytes 2359304 | tf_op jit(solution)/shard_map/ppermute | solution.py:146
  591.1 192.5 %all-gather.17.cloned.1.call-start = ((), (), s32[]{:S(2)}) async-start(), calls=%async_computation.5 | async-start | bytes 14155776 | tf_op jit(solution)/shard_map/all_gather | solution.py:239
  647.0 59.7 %collective-permute-start.39 = (bf16[96,4096]{1,0:T(8,128)(2,1)}, bf16[96,4096]{1,0:T(8,128)(2,1)S(1)}, u32[]{:S(2)}, u32[]{:S(2)}) collective-permute-start(bf16[96,4096]{1,0:T(8,128)(2,1)} %get-tuple-element.317), channel_id=1, source_target_pairs={{0,6},{1,7},{2,0},{3,1},{4,2},{5,3},{6,4},{7,5},{8,14},{9,15},{10,... | collective-permute-start | bytes 2359304 | tf_op jit(solution)/shard_map/ppermute | solution.py:146
  649.0 57.7 %collective-permute-start.41 = (bf16[96,4096]{1,0:T(8,128)(2,1)}, bf16[96,4096]{1,0:T(8,128)(2,1)}, u32[]{:S(2)}, u32[]{:S(2)}) collective-permute-start(bf16[96,4096]{1,0:T(8,128)(2,1)} %get-tuple-element.316), channel_id=1, source_target_pairs={{0,2},{1,3},{2,4},{3,5},{4,6},{5,7},{6,0},{7,1},{8,10},{9,11},{10,... | collective-permute-start | bytes 2359304 | tf_op jit(solution)/shard_map/ppermute | solution.py:146
  713.7 63.1 %collective-permute-start.36 = (bf16[768,4096]{1,0:T(8,128)(2,1)}, bf16[768,4096]{1,0:T(8,128)(2,1)S(1)}, u32[]{:S(2)}, u32[]{:S(2)}) collective-permute-start(bf16[768,4096]{1,0:T(8,128)(2,1)} %convolution_convert_fusion.11), channel_id=1, source_target_pairs={{0,1},{1,0},{2,3},{3,2},{4,5},{5,4},{6,7},{7,6},{8,9},{9,8},{10,11... | collective-permute-start | bytes 18874376 | tf_op jit(solution)/shard_map/ppermute | solution.py:146
  730.6 82.3 %collective-permute-start.46 = (bf16[768,4096]{1,0:T(8,128)(2,1)}, bf16[768,4096]{1,0:T(8,128)(2,1)}, u32[]{:S(2)}, u32[]{:S(2)}) collective-permute-start(bf16[768,4096]{1,0:T(8,128)(2,1)} %convolution_convert_fusion.9), channel_id=1, source_target_pairs={{0,1},{1,0},{2,3},{3,2},{4,5},{5,4},{6,7},{7,6},{8,9},{9,8},{10,11... | collective-permute-start | bytes 18874376 | tf_op jit(solution)/shard_map/ppermute | solution.py:146
  780.4 40.0 %collective-permute-start.44 = (bf16[96,4096]{1,0:T(8,128)(2,1)}, bf16[96,4096]{1,0:T(8,128)(2,1)}, u32[]{:S(2)}, u32[]{:S(2)}) collective-permute-start(bf16[96,4096]{1,0:T(8,128)(2,1)} %get-tuple-element.311), channel_id=1, source_target_pairs={{0,2},{1,3},{2,4},{3,5},{4,6},{5,7},{6,0},{7,1},{8,10},{9,11},{10,... | collective-permute-start | bytes 2359304 | tf_op jit(solution)/shard_map/ppermute | solution.py:146
  781.0 41.3 %collective-permute-start.45 = (bf16[96,4096]{1,0:T(8,128)(2,1)}, bf16[96,4096]{1,0:T(8,128)(2,1)}, u32[]{:S(2)}, u32[]{:S(2)}) collective-permute-start(bf16[96,4096]{1,0:T(8,128)(2,1)} %get-tuple-element.310), channel_id=1, source_target_pairs={{0,6},{1,7},{2,0},{3,1},{4,2},{5,3},{6,4},{7,5},{8,14},{9,15},{10,... | collective-permute-start | bytes 2359304 | tf_op jit(solution)/shard_map/ppermute | solution.py:146
  817.0 54.0 %collective-permute-start.50 = (bf16[96,4096]{1,0:T(8,128)(2,1)}, bf16[96,4096]{1,0:T(8,128)(2,1)}, u32[]{:S(2)}, u32[]{:S(2)}) collective-permute-start(bf16[96,4096]{1,0:T(8,128)(2,1)} %get-tuple-element.307), channel_id=1, source_target_pairs={{0,2},{1,3},{2,4},{3,5},{4,6},{5,7},{6,0},{7,1},{8,10},{9,11},{10,... | collective-permute-start | bytes 2359304 | tf_op jit(solution)/shard_map/ppermute | solution.py:146
  817.1 54.0 %collective-permute-start.51 = (bf16[96,4096]{1,0:T(8,128)(2,1)S(1)}, bf16[96,4096]{1,0:T(8,128)(2,1)}, u32[]{:S(2)}, u32[]{:S(2)}) collective-permute-start(bf16[96,4096]{1,0:T(8,128)(2,1)S(1)} %get-tuple-element.306), channel_id=1, source_target_pairs={{0,6},{1,7},{2,0},{3,1},{4,2},{5,3},{6,4},{7,5},{8,14},{9,15},{10,... | collective-permute-start | bytes 2359304 | tf_op jit(solution)/shard_map/ppermute | solution.py:146
  820.3 75.0 %collective-permute-start.53 = (bf16[96,4096]{1,0:T(8,128)(2,1)}, bf16[96,4096]{1,0:T(8,128)(2,1)}, u32[]{:S(2)}, u32[]{:S(2)}) collective-permute-start(bf16[96,4096]{1,0:T(8,128)(2,1)} %get-tuple-element.304), channel_id=1, source_target_pairs={{0,6},{1,7},{2,0},{3,1},{4,2},{5,3},{6,4},{7,5},{8,14},{9,15},{10,... | collective-permute-start | bytes 2359304 | tf_op jit(solution)/shard_map/ppermute | solution.py:146
  820.3 75.0 %collective-permute-start.55 = (bf16[96,4096]{1,0:T(8,128)(2,1)}, bf16[96,4096]{1,0:T(8,128)(2,1)}, u32[]{:S(2)}, u32[]{:S(2)}) collective-permute-start(bf16[96,4096]{1,0:T(8,128)(2,1)} %get-tuple-element.305), channel_id=1, source_target_pairs={{0,2},{1,3},{2,4},{3,5},{4,6},{5,7},{6,0},{7,1},{8,10},{9,11},{10,... | collective-permute-start | bytes 2359304 | tf_op jit(solution)/shard_map/ppermute | solution.py:146
  842.1 62.8 %collective-permute-start.52 = (bf16[768,4096]{1,0:T(8,128)(2,1)}, bf16[768,4096]{1,0:T(8,128)(2,1)S(1)}, u32[]{:S(2)}, u32[]{:S(2)}) collective-permute-start(bf16[768,4096]{1,0:T(8,128)(2,1)} %convolution_convert_fusion.7), channel_id=1, source_target_pairs={{0,1},{1,0},{2,3},{3,2},{4,5},{5,4},{6,7},{7,6},{8,9},{9,8},{10,11... | collective-permute-start | bytes 18874376 | tf_op jit(solution)/shard_map/ppermute | solution.py:146
  897.3 36.6 %collective-permute-start.47 = (bf16[96,4096]{1,0:T(8,128)(2,1)}, bf16[96,4096]{1,0:T(8,128)(2,1)S(1)}, u32[]{:S(2)}, u32[]{:S(2)}) collective-permute-start(bf16[96,4096]{1,0:T(8,128)(2,1)} %get-tuple-element.303), channel_id=1, source_target_pairs={{0,2},{1,3},{2,4},{3,5},{4,6},{5,7},{6,0},{7,1},{8,10},{9,11},{10,... | collective-permute-start | bytes 2359304 | tf_op jit(solution)/shard_map/ppermute | solution.py:146
  897.4 37.2 %collective-permute-start.49 = (bf16[96,4096]{1,0:T(8,128)(2,1)}, bf16[96,4096]{1,0:T(8,128)(2,1)S(1)}, u32[]{:S(2)}, u32[]{:S(2)}) collective-permute-start(bf16[96,4096]{1,0:T(8,128)(2,1)} %get-tuple-element.302), channel_id=1, source_target_pairs={{0,6},{1,7},{2,0},{3,1},{4,2},{5,3},{6,4},{7,5},{8,14},{9,15},{10,... | collective-permute-start | bytes 2359304 | tf_op jit(solution)/shard_map/ppermute | solution.py:146
  907.2 43.6 %collective-permute-start.58 = (bf16[96,4096]{1,0:T(8,128)(2,1)}, bf16[96,4096]{1,0:T(8,128)(2,1)S(1)}, u32[]{:S(2)}, u32[]{:S(2)}) collective-permute-start(bf16[96,4096]{1,0:T(8,128)(2,1)} %get-tuple-element.299), channel_id=1, source_target_pairs={{0,2},{1,3},{2,4},{3,5},{4,6},{5,7},{6,0},{7,1},{8,10},{9,11},{10,... | collective-permute-start | bytes 2359304 | tf_op jit(solution)/shard_map/ppermute | solution.py:146
  915.7 35.0 %collective-permute-start.59 = (bf16[96,4096]{1,0:T(8,128)(2,1)S(1)}, bf16[96,4096]{1,0:T(8,128)(2,1)S(1)}, u32[]{:S(2)}, u32[]{:S(2)}) collective-permute-start(bf16[96,4096]{1,0:T(8,128)(2,1)S(1)} %get-tuple-element.298), channel_id=1, source_target_pairs={{0,6},{1,7},{2,0},{3,1},{4,2},{5,3},{6,4},{7,5},{8,14},{9,15},{10,... | collective-permute-start | bytes 2359304 | tf_op jit(solution)/shard_map/ppermute | solution.py:146
  917.0 49.2 %collective-permute-start.57 = (bf16[96,4096]{1,0:T(8,128)(2,1)S(1)}, bf16[96,4096]{1,0:T(8,128)(2,1)S(1)}, u32[]{:S(2)}, u32[]{:S(2)}) collective-permute-start(bf16[96,4096]{1,0:T(8,128)(2,1)S(1)} %get-tuple-element.297), channel_id=1, source_target_pairs={{0,6},{1,7},{2,0},{3,1},{4,2},{5,3},{6,4},{7,5},{8,14},{9,15},{10,... | collective-permute-start | bytes 2359304 | tf_op jit(solution)/shard_map/ppermute | solution.py:146
  933.9 33.7 %collective-permute-start.61 = (bf16[96,4096]{1,0:T(8,128)(2,1)S(1)}, bf16[96,4096]{1,0:T(8,128)(2,1)S(1)}, u32[]{:S(2)}, u32[]{:S(2)}) collective-permute-start(bf16[96,4096]{1,0:T(8,128)(2,1)S(1)} %get-tuple-element.296), channel_id=1, source_target_pairs={{0,2},{1,3},{2,4},{3,5},{4,6},{5,7},{6,0},{7,1},{8,10},{9,11},{10,... | collective-permute-start | bytes 2359304 | tf_op jit(solution)/shard_map/ppermute | solution.py:146
  (100 other events, 2303.7 us)
Sparse Core Ops, SparseCore 0:
  129.0 108.5 all-gather.6
  239.2 62.9 all-gather.8
  384.9 92.4 all-gather.10
  478.9 110.6 all-gather.12
  591.2 74.4 all-gather.14
  713.8 63.2 all-gather.16
